TPU v7x, 32 devices: a whole 2x2x4 slice. The times are simulated.
32 devices in a mesh: blk: 16 (over z, y, core), along: 2 (over x).
Axes of the slice: x: 2, y: 2, z: 4, core: 2. Of those that a mesh axis runs over, the one named last changes fastest.
Arguments:
- values: float32 [3, 16, 48, 256], P(None, 'blk', 'along'), may hold values from -6 to 6
- offsets: float32 [3, 16, 48, 256], P(None, 'blk', 'along'), may hold values from 0 to 1
- stiffness: float32 [16, 48, 256], P('blk', 'along'), may hold values from 0.5 to 2
- leaf_basis: float32 [16, 48, 64, 256], P('blk', 'along'), may hold values from -0.375 to 0.375
- transfer: float32 [16, 48, 64, 64], P('blk', 'along'), may hold values from -0.15625 to 0.15625
- slab_transfer_matrices: float32 [16, 2, 64, 64], P('blk', 'along'), may hold values from -0.5 to 0.5
- leaf_coupling_matrices: float32 [16, 30, 64, 64], P('blk'), may hold values from -0.375 to 0.375
- leaf_admissible_mask: int32 [16, 30], P('blk'), may hold values 0 or 1
- top_coupling: float32 [16, 16, 64, 64], P('blk'), may hold values from -0.75 to 0.75
- top_admissible: int32 [16, 16], P('blk'), may hold values 0 or 1
Outputs:
- product: float32 [3, 16, 48, 256], P(None, 'blk', 'along')
All inputs are finite; a program needn't handle non-finite values. No bound on the sum of `leaf_admissible_mask` or of `top_admissible` on one device may be relied on, other than what follows from the above.
Results may differ from a plain program's by a relative error of at most 0.0001.
Values sent between devices are 32-bit elements; how exact they have to be, the bound alone decides.
A program may use at most 64 MiB of HBM per device.

v0:
```python
import jax
import jax.numpy as jnp
from jax import lax
from jax.sharding import PartitionSpec as P

REACH = 6


SHARPNESS = 2.0
KERNEL_SCALE = 0.125
HIGHEST_ACCURACY = lax.Precision.HIGHEST


def with_halo(cells, sides, width, closed):
    for axis, dim in sides:
        count = lax.axis_size(axis)
        ends = count if closed else count - 1
        head = lax.slice_in_dim(cells, 0, width, axis=dim)
        tail = lax.slice_in_dim(cells, cells.shape[dim] - width, cells.shape[dim], axis=dim)
        cells = jnp.concatenate(
            [
                lax.ppermute(tail, axis, [(i, (i + 1) % count) for i in range(ends)]),
                cells,
                lax.ppermute(head, axis, [((i + 1) % count, i) for i in range(ends)]),
            ],
            axis=dim,
        )
    return cells


def passed_along(x, axis, by):
    count = lax.axis_size(axis)
    return lax.ppermute(x, axis, [(i, (i + by) % count) for i in range(count)])


def near_field(padded):
    leaves = padded.shape[2] - 2
    center = padded[:, 1:2, 1 : 1 + leaves]
    result = jnp.zeros((3, 1, leaves, padded.shape[3]), jnp.float32)
    for around in (-1, 0, 1):
        for along_step in (-1, 0, 1):
            source = padded[:, 1 + around : 2 + around, 1 + along_step : 1 + along_step + leaves]
            gap_around = around + source[0][..., None, :] - center[0][..., :, None]
            gap_along = along_step + source[1][..., None, :] - center[1][..., :, None]
            gap_radial = source[2][..., None, :] - center[2][..., :, None]
            squared = gap_around * gap_around + gap_along * gap_along + gap_radial * gap_radial
            kernel = (
                KERNEL_SCALE
                * center[3][..., :, None]
                * source[3][..., None, :]
                * jnp.exp(-SHARPNESS * squared)
            )
            result = result + jnp.einsum(
                "alij,ralj->rali", kernel, source[4:], precision=HIGHEST_ACCURACY
            )
    return result


def slot_number(around, along_step, reach):
    block = around - 2 if around > 0 else reach - 1 + (-around - 2)
    return 3 * block + along_step + 1


def add_sector(total, held, around, leaf_coupling_matrices, leaf_admissible_mask):
    leaves = total.shape[2]
    for along_step in (-1, 0, 1):
        slot = slot_number(around, along_step, REACH)
        partner = held[:, :, 1 + along_step : 1 + along_step + leaves]
        coupling = (
            leaf_coupling_matrices[:, slot]
            * leaf_admissible_mask[:, slot].astype(jnp.float32)[:, None, None]
        )
        total = total + jnp.einsum("skq,rslq->rslk", coupling, partner, precision=HIGHEST_ACCURACY)
    return total


def body(
    values,
    offsets,
    stiffness,
    leaf_basis,
    transfer,
    slab_transfer_matrices,
    leaf_coupling_matrices,
    leaf_admissible_mask,
    top_coupling,
    top_admissible,
):
    stacked = jnp.concatenate([offsets, stiffness[None], values], 0)
    padded = with_halo(stacked, (("blk", 1), ("along", 2)), 1, True)
    at_start = lax.axis_index("along") == 0
    at_finish = lax.axis_index("along") == lax.axis_size("along") - 1
    lower_rim = jnp.where(at_start, 0.0, padded[:, :, :1])
    upper_rim = jnp.where(at_finish, 0.0, padded[:, :, -1:])
    padded = jnp.concatenate([lower_rim, padded[:, :, 1:-1], upper_rim], 2)
    near = near_field(padded)
    coefs = jnp.einsum("slki,rsli->rslk", leaf_basis, values, precision=HIGHEST_ACCURACY)
    rimmed = with_halo(coefs, (("along", 2),), 1, False)
    far_leaf = jnp.zeros(coefs.shape, jnp.float32)
    sectors = lax.axis_size("blk")
    lower_window = rimmed
    upper_window = rimmed
    breadth = 1
    while breadth <= REACH:
        lower_came = passed_along(lower_window, "blk", breadth)
        upper_came = passed_along(upper_window, "blk", -breadth)
        lower_window = jnp.concatenate([lower_window, lower_came], 1)
        upper_window = jnp.concatenate([upper_window, upper_came], 1)
        breadth = 2 * breadth
    for distance in range(2, REACH + 1):
        far_leaf = add_sector(
            far_leaf,
            lower_window[:, distance : distance + 1],
            -distance,
            leaf_coupling_matrices,
            leaf_admissible_mask,
        )
        far_leaf = add_sector(
            far_leaf,
            upper_window[:, distance : distance + 1],
            distance,
            leaf_coupling_matrices,
            leaf_admissible_mask,
        )
    slab_coefficient_rows = jnp.einsum(
        "slqk,rslq->rsk", transfer, coefs, precision=HIGHEST_ACCURACY
    )
    shared_portion = jnp.einsum(
        "oxz,eox->eoz",
        slab_transfer_matrices[:, 0],
        slab_coefficient_rows,
        precision=HIGHEST_ACCURACY,
    )
    sector_coefs = lax.psum(shared_portion, "along")
    every_sector = lax.all_gather(sector_coefs, "blk", axis=1, tiled=True)
    sector = lax.axis_index("blk")
    others = jnp.arange(sectors, dtype=jnp.int32)
    apart = (others - sector) % sectors
    distant = jnp.logical_and(apart > REACH, apart < sectors - REACH).astype(jnp.float32)
    allowed = top_admissible[0].astype(jnp.float32) * distant
    sector_local_coefs = jnp.einsum(
        "stkq,rtq->rsk",
        top_coupling * allowed[None, :, None, None],
        every_sector,
        precision=HIGHEST_ACCURACY,
    )
    slab_local_coefs = jnp.einsum(
        "baz,lbz->lba", slab_transfer_matrices[:, 0], sector_local_coefs, precision=HIGHEST_ACCURACY
    )
    leaf_down = jnp.einsum("slqk,rsk->rslq", transfer, slab_local_coefs, precision=HIGHEST_ACCURACY)
    leaf_local = far_leaf + leaf_down
    return near + jnp.einsum("slki,rslk->rsli", leaf_basis, leaf_local, precision=HIGHEST_ACCURACY)


def solution(mesh):
    return jax.shard_map(
        body,
        mesh=mesh,
        in_specs=(
            P(None, "blk", "along", None),
            P(None, "blk", "along", None),
            P("blk", "along", None),
            P("blk", "along", None, None),
            P("blk", "along", None, None),
            P("blk", "along", None, None),
            P("blk", None, None, None),
            P("blk", None),
            P("blk", None, None, None),
            P("blk", None),
        ),
        out_specs=P(None, "blk", "along", None),
        check_vma=False,
    )
```

profile of v0, /device:TPU:0, one launch (start us, length us, event | category | flops | bytes accessed | tf_op | source)
XLA Modules:
  0.0 189.9 jit_solution(18029766824902312547)
XLA Ops:
  0.0 1.1 copy.17
  1.1 0.8 broadcast_in_dim.8
  1.9 0.9 copy.16
  3.5 5.5 %collective-permute-start.1 = (f32[7,1,24,256]{3,0,2,1:T(8,128)}, f32[7,1,24,256]{3,0,2,1:T(8,128)S(1)}, u32[]{:S(2)}, u32[]{:S(2)}) collective-permute-start(f32[7,1,24,256]{3,0,2,1:T(8,128)} %pad_maximum_fusion.4), channel_id=1, source_target_pairs={{2,0},{4,2},{6,4},{8,6},{10,8},{12,10},{14,12},{16,14},{18,16},{20... | collective-permute-start | bytes 516104 | tf_op jit(solution)/shard_map/ppermute | solution.py:24
  9.0 2.3 %fusion.200 = f32[24,3,64]{2,1,0:T(4,128)S(1)} fusion(f32[1,24,64,256]{3,2,1,0:T(8,128)S(1)} %copy-done, f32[3,24,256]{2,1,0:T(8,128)} %bitcast.397), kind=kOutput, calls=%fused_computation.200 | convolution fusion | flops 14155776 | bytes 1665024 | tf_op jit(solution)/shard_map/slki,rsli->rslk/dot_general | solution.py:97
  11.9 1.3 collective-permute-start.5
  13.2 5.1 %collective-permute-start.4 = (f32[3,1,1,64]{3,0,2,1:T(4,128)}, f32[3,1,1,64]{3,0,2,1:T(4,128)}, u32[]{:S(2)}, u32[]{:S(2)}) collective-permute-start(f32[3,1,1,64]{3,0,2,1:T(4,128)} %get-tuple-element.78), channel_id=1, source_target_pairs={{0,1},{2,3},{4,5},{6,7},{8,9},{10,11},{12,13},{14,15},{16,17},{18,... | collective-permute-start | bytes 2312 | tf_op jit(solution)/shard_map/ppermute | solution.py:22
  20.8 5.6 %psum.7 = f32[3,1,64]{2,0,1:T(4,128)} all-reduce(f32[3,1,64]{2,0,1:T(4,128)} %convolution_bitcast_fusion.2), channel_id=1, replica_groups=mesh['blk'=16,'along'=2] {'along'}, use_global_device_ids=true, to_apply=%region_0.1 | all-reduce | flops 192 | bytes 1536 | tf_op jit(solution)/shard_map/psum | solution.py:134
  26.5 19.9 %all_gather.3 = f32[3,16,64]{2,0,1:T(4,128)} all-gather(f32[3,1,64]{2,0,1:T(4,128)} %psum.7), channel_id=1, replica_groups=mesh['blk'=16,'along'=2] {'blk'}, dimensions={1}, use_global_device_ids=true | all-gather | bytes 13056 | tf_op jit(solution)/shard_map/all_gather | solution.py:135
  47.0 1.3 convolution_bitcast_fusion
  48.3 0.9 convolution_bitcast_fusion.1
  50.4 4.1 %collective-permute-start.8 = (f32[3,1,26,64]{3,0,2,1:T(4,128)S(1)}, f32[3,1,26,64]{3,0,2,1:T(4,128)S(1)}, u32[]{:S(2)}, u32[]{:S(2)}) collective-permute-start(f32[3,1,26,64]{3,0,2,1:T(4,128)S(1)} %pad_maximum_fusion.8), channel_id=1, source_target_pairs={{0,30},{2,0},{4,2},{6,4},{8,6},{10,8},{12,10},{14,12},{16,14},{18,... | collective-permute-start | bytes 59912 | tf_op jit(solution)/shard_map/ppermute | solution.py:33
  55.2 1.1 collective-permute-done.6
  56.3 1.4 pad_maximum_fusion.5
  57.7 4.7 %collective-permute-start.9 = (f32[3,2,26,64]{3,0,2,1:T(4,128)S(1)}, f32[3,2,26,64]{3,0,2,1:T(4,128)S(1)}, u32[]{:S(2)}, u32[]{:S(2)}) collective-permute-start(f32[3,2,26,64]{3,0,2,1:T(4,128)S(1)} %get-tuple-element.77), channel_id=1, source_target_pairs={{0,28},{2,30},{4,0},{6,2},{8,4},{10,6},{12,8},{14,10},{16,12},{18,... | collective-permute-start | bytes 119816 | tf_op jit(solution)/shard_map/ppermute | solution.py:33
  82.0 0.8 pad_maximum_fusion.1
  82.9 2.0 %collective-permute-start.10 = (f32[3,4,26,64]{3,0,2,1:T(4,128)S(1)}, f32[3,4,26,64]{3,0,2,1:T(4,128)S(1)}, u32[]{:S(2)}, u32[]{:S(2)}) collective-permute-start(f32[3,4,26,64]{3,0,2,1:T(4,128)S(1)} %get-tuple-element.74), channel_id=1, source_target_pairs={{0,8},{2,10},{4,12},{6,14},{8,16},{10,18},{12,20},{14,22},{16,24},... | collective-permute-start | bytes 239624 | tf_op jit(solution)/shard_map/ppermute | solution.py:33
  84.9 1.0 fusion.279
  88.4 6.1 %collective-permute-done.11 = f32[3,4,26,64]{3,0,2,1:T(4,128)S(1)} collective-permute-done((f32[3,4,26,64]{3,0,2,1:T(4,128)S(1)}, f32[3,4,26,64]{3,0,2,1:T(4,128)S(1)}, u32[]{:S(2)}, u32[]{:S(2)}) %collective-permute-start.11) | collective-permute-done | bytes 79904 | tf_op jit(solution)/shard_map/ppermute | solution.py:33
  98.7 2.0 %convolution_add_fusion = f32[3,24,64]{2,0,1:T(4,128)S(1)} fusion(f32[3,64,1]{1,0,2:T(4,128)S(1)} %convolution_bitcast_fusion.1, f32[1,24,64,64]{3,2,1,0:T(8,128)S(1)} %copy-done.1, f32[3,24,64]{2,1,0:T(8,128)S(1)} %fusion.243, f32[3,24,64]{2,1,0:T(8,128)S(1)} %fusion.245, f32[3,24,64]{2,1,0:T(8,128)S(1)} %fusion.247, f32[3,24,64]{2,1,0:T(8,128)S(1)} %fusion.249, ...), kind=kOutput, calls=%fused_computation.213 | convolution fusion | flops 3677184 | bytes 965376 | tf_op jit(solution)/shard_map/slqk,rsk->rslq/dot_general | solution.py:150
  100.6 2.0 %collective-permute-start.2 = (f32[7,3,1,256]{3,0,2,1:T(8,128)S(1)}, f32[7,3,1,256]{3,0,2,1:T(8,128)S(1)}, u32[]{:S(2)}, u32[]{:S(2)}) collective-permute-start(f32[7,3,1,256]{3,0,2,1:T(8,128)S(1)} %get-tuple-element.31), channel_id=1, source_target_pairs={{0,1},{1,0},{2,3},{3,2},{4,5},{5,4},{6,7},{7,6},{8,9},{9,8},{10,11... | collective-permute-start | bytes 64520 | tf_op jit(solution)/shard_map/ppermute | solution.py:22
  102.9 1.6 collective-permute-done.2
  106.3 9.2 %fusion = f32[24,3,256]{2,1,0:T(4,128)S(1)} fusion(f32[24,256]{1,0:T(8,128)S(1)} %get-tuple-element.110, f32[24,256]{1,0:T(8,128)S(1)} %get-tuple-element.111, f32[24,256]{1,0:T(8,128)S(1)} %get-tuple-element.112, f32[24,256]{1,0:T(8,128)S(1)} %get-tuple-element.113, f32[24,256]{1,0:T(8,128)S(1)} %copy-done.11, f32[24,256]{1,0:T(8,128)S(1)} %copy-done.12, ...), kind=kOutput, calls=%fused_computation | convolution fusion | flops 73924608 | bytes 368640 | tf_op jit(solution)/shard_map/alij,ralj->rali/dot_general | solution.py:53
  115.5 9.1 %fusion.39 = f32[24,3,256]{2,1,0:T(4,128)S(1)} fusion(f32[24,256]{1,0:T(8,128)S(1)} %get-tuple-element.122, f32[24,256]{1,0:T(8,128)S(1)} %get-tuple-element.123, f32[24,256]{1,0:T(8,128)S(1)} %get-tuple-element.124, f32[24,256]{1,0:T(8,128)S(1)} %get-tuple-element.125, f32[24,256]{1,0:T(8,128)S(1)} %copy-done.11, f32[24,256]{1,0:T(8,128)S(1)} %copy-done.12, ...), kind=kOutput, calls=%fused_computation.39 | convolution fusion | flops 73924608 | bytes 368640 | tf_op jit(solution)/shard_map/alij,ralj->rali/dot_general | solution.py:53
  124.5 9.1 %fusion.26 = f32[24,3,256]{2,1,0:T(4,128)S(1)} fusion(f32[24,256]{1,0:T(8,128)S(1)} %get-tuple-element.114, f32[24,256]{1,0:T(8,128)S(1)} %get-tuple-element.115, f32[24,256]{1,0:T(8,128)S(1)} %get-tuple-element.118, f32[24,256]{1,0:T(8,128)S(1)} %get-tuple-element.119, f32[24,256]{1,0:T(8,128)S(1)} %copy-done.11, f32[24,256]{1,0:T(8,128)S(1)} %copy-done.12, ...), kind=kOutput, calls=%fused_computation.26 | convolution fusion | flops 73924608 | bytes 368640 | tf_op jit(solution)/shard_map/alij,ralj->rali/dot_general | solution.py:53
  133.6 9.1 %fusion.65 = f32[24,3,256]{2,1,0:T(4,128)S(1)} fusion(f32[24,256]{1,0:T(8,128)S(1)} %get-tuple-element.126, f32[24,256]{1,0:T(8,128)S(1)} %get-tuple-element.127, f32[24,256]{1,0:T(8,128)S(1)} %get-tuple-element.130, f32[24,256]{1,0:T(8,128)S(1)} %get-tuple-element.131, f32[24,256]{1,0:T(8,128)S(1)} %copy-done.11, f32[24,256]{1,0:T(8,128)S(1)} %copy-done.12, ...), kind=kOutput, calls=%fused_computation.65 | convolution fusion | flops 73924608 | bytes 368640 | tf_op jit(solution)/shard_map/alij,ralj->rali/dot_general | solution.py:53
  142.6 9.1 %fusion.78 = f32[24,3,256]{2,1,0:T(4,128)S(1)} fusion(f32[24,256]{1,0:T(8,128)S(1)} %get-tuple-element.134, f32[24,256]{1,0:T(8,128)S(1)} %get-tuple-element.135, f32[24,256]{1,0:T(8,128)S(1)} %get-tuple-element.136, f32[24,256]{1,0:T(8,128)S(1)} %get-tuple-element.137, f32[24,256]{1,0:T(8,128)S(1)} %copy-done.11, f32[24,256]{1,0:T(8,128)S(1)} %copy-done.12, ...), kind=kOutput, calls=%fused_computation.78 | convolution fusion | flops 73924608 | bytes 368640 | tf_op jit(solution)/shard_map/alij,ralj->rali/dot_general | solution.py:53
  151.7 9.1 %fusion.104 = f32[24,3,256]{2,1,0:T(4,128)S(1)} fusion(f32[24,256]{1,0:T(8,128)S(1)} %copy-done.11, f32[24,256]{1,0:T(8,128)S(1)} %get-tuple-element.133, f32[24,256]{1,0:T(8,128)S(1)} %copy-done.12, f32[24,256]{1,0:T(8,128)S(1)} %get-tuple-element.129, f32[24,256]{1,0:T(8,128)S(1)} %copy-done.10, f32[24,256]{1,0:T(8,128)S(1)} %get-tuple-element.121, ...), kind=kOutput, calls=%fused_computation.104 | convolution fusion | flops 73924608 | bytes 368640 | tf_op jit(solution)/shard_map/alij,ralj->rali/dot_general | solution.py:53
  160.8 9.1 %fusion.226 = f32[24,3,256]{2,1,0:T(4,128)S(1)} fusion(f32[24,3,256]{2,1,0:T(4,128)S(1)} %fusion.65, f32[24,3,256]{2,1,0:T(4,128)S(1)} %fusion.78, f32[24,3,256]{2,1,0:T(4,128)S(1)} %fusion.104, f32[24,256]{1,0:T(8,128)S(1)} %get-tuple-element.116, f32[24,256]{1,0:T(8,128)S(1)} %get-tuple-element.120, f32[24,256]{1,0:T(8,128)S(1)} %get-tuple-element.128, ...), kind=kOutput, calls=%fused_computation.210 | convolution fusion | flops 73979904 | bytes 663552 | tf_op jit(solution)/shard_map/alij,ralj->rali/dot_general | solution.py:53
  169.9 9.5 %fusion.217 = f32[24,3,256]{2,1,0:T(4,128)S(1)} fusion(f32[24,3,256]{2,1,0:T(4,128)S(1)} %fusion.26, f32[24,3,256]{2,1,0:T(4,128)S(1)} %fusion.39, f32[24,3,256]{2,1,0:T(4,128)S(1)} %fusion.226, f32[24,256]{1,0:T(8,128)S(1)} %copy-done.11, f32[24,256]{1,0:T(8,128)S(1)} %copy-done.12, f32[24,256]{1,0:T(8,128)S(1)} %copy-done.10, ...), kind=kOutput, calls=%fused_computation.207 | convolution fusion | flops 73979904 | bytes 491520 | tf_op jit(solution)/shard_map/alij,ralj->rali/dot_general | solution.py:53
  179.3 9.1 %fusion.232 = f32[24,3,256]{2,1,0:T(4,128)S(1)} fusion(f32[24,3,256]{2,1,0:T(4,128)S(1)} %fusion, f32[24,3,256]{2,1,0:T(4,128)S(1)} %fusion.217, f32[24,256]{1,0:T(8,128)S(1)} %get-tuple-element.138, f32[24,256]{1,0:T(8,128)S(1)} %get-tuple-element.139, f32[24,256]{1,0:T(8,128)S(1)} %get-tuple-element.140, f32[24,256]{1,0:T(8,128)S(1)} %get-tuple-element.141, ...), kind=kOutput, calls=%fused_computation.212 | convolution fusion | flops 73961472 | bytes 565248 | tf_op jit(solution)/shard_map/alij,ralj->rali/dot_general | solution.py:53
  188.4 0.9 fusion.205
  (114 shorter events, 16.1 us)
Async XLA Ops:
  0.0 9.0 %copy-start = (f32[1,24,64,256]{3,2,1,0:T(8,128)S(1)}, f32[1,24,64,256]{3,2,1,0:T(8,128)}, u32[]{:S(2)}) copy-start(f32[1,24,64,256]{3,2,1,0:T(8,128)} %param.13) | copy-start | bytes 4718596
  0.0 19.0 %copy-start.8 = (f32[1,24,256]{2,1,0:T(8,128)S(1)}, f32[1,24,256]{2,1,0:T(8,128)}, u32[]{:S(2)}) copy-start(f32[1,24,256]{2,1,0:T(8,128)} %param.12) | copy-start | bytes 73732
  0.0 18.3 %copy-start.6 = (f32[3,1,24,256]{3,2,1,0:T(8,128)S(1)}, f32[3,1,24,256]{3,2,1,0:T(8,128)}, u32[]{:S(2)}) copy-start(f32[3,1,24,256]{3,2,1,0:T(8,128)} %param.11) | copy-start | bytes 221188
  0.0 19.6 %copy-start.1 = (f32[1,24,64,64]{3,2,1,0:T(8,128)S(1)}, f32[1,24,64,64]{3,2,1,0:T(8,128)}, u32[]{:S(2)}) copy-start(f32[1,24,64,64]{3,2,1,0:T(8,128)} %param.14) | copy-start | bytes 1179652
  2.8 17.3 %copy-start.7 = (f32[1,1,64,64]{3,2,1,0:T(8,128)S(1)}, f32[1,1,64,64]{3,2,1,0:T(8,128)}, u32[]{:S(2)}) copy-start(f32[1,1,64,64]{3,2,1,0:T(8,128)} %param.15) | copy-start | bytes 49156
  2.8 44.2 %copy-start.3 = (f32[1,16,64,64]{3,2,1,0:T(8,128)S(1)}, f32[1,16,64,64]{3,2,1,0:T(8,128)}, u32[]{:S(2)}) copy-start(f32[1,16,64,64]{3,2,1,0:T(8,128)} %param.18) | copy-start | bytes 786436
  3.5 95.0 %collective-permute-start.1 = (f32[7,1,24,256]{3,0,2,1:T(8,128)}, f32[7,1,24,256]{3,0,2,1:T(8,128)S(1)}, u32[]{:S(2)}, u32[]{:S(2)}) collective-permute-start(f32[7,1,24,256]{3,0,2,1:T(8,128)} %pad_maximum_fusion.4), channel_id=1, source_target_pairs={{2,0},{4,2},{6,4},{8,6},{10,8},{12,10},{14,12},{16,14},{18,16},{20... | collective-permute-start | bytes 516104 | tf_op jit(solution)/shard_map/ppermute | solution.py:24
  9.0 89.5 %collective-permute-start = (f32[7,1,24,256]{3,0,2,1:T(8,128)}, f32[7,1,24,256]{3,0,2,1:T(8,128)S(1)}, u32[]{:S(2)}, u32[]{:S(2)}) collective-permute-start(f32[7,1,24,256]{3,0,2,1:T(8,128)} %pad_maximum_fusion.4), channel_id=1, source_target_pairs={{0,2},{2,4},{4,6},{6,8},{8,10},{10,12},{12,14},{14,16},{16,18},{18... | collective-permute-start | bytes 516104 | tf_op jit(solution)/shard_map/ppermute | solution.py:22
  9.0 45.4 %copy-start.4 = (s32[1,30]{1,0:T(1,128)S(1)}, s32[1,30]{1,0:T(1,128)}, u32[]{:S(2)}) copy-start(s32[1,30]{1,0:T(1,128)} %param.17) | copy-start | bytes 364
  11.9 37.3 %collective-permute-start.5 = (f32[3,1,1,64]{3,0,2,1:T(4,128)}, f32[3,1,1,64]{3,0,2,1:T(4,128)S(1)}, u32[]{:S(2)}, u32[]{:S(2)}) collective-permute-start(f32[3,1,1,64]{3,0,2,1:T(4,128)} %get-tuple-element.79), channel_id=1, source_target_pairs={{1,0},{3,2},{5,4},{7,6},{9,8},{11,10},{13,12},{15,14},{17,16},{19,... | collective-permute-start | bytes 2312 | tf_op jit(solution)/shard_map/ppermute | solution.py:24
  13.2 36.1 %collective-permute-start.4 = (f32[3,1,1,64]{3,0,2,1:T(4,128)}, f32[3,1,1,64]{3,0,2,1:T(4,128)}, u32[]{:S(2)}, u32[]{:S(2)}) collective-permute-start(f32[3,1,1,64]{3,0,2,1:T(4,128)} %get-tuple-element.78), channel_id=1, source_target_pairs={{0,1},{2,3},{4,5},{6,7},{8,9},{10,11},{12,13},{14,15},{16,17},{18,... | collective-permute-start | bytes 2312 | tf_op jit(solution)/shard_map/ppermute | solution.py:22
  50.0 6.3 %collective-permute-start.6 = (f32[3,1,26,64]{3,0,2,1:T(4,128)S(1)}, f32[3,1,26,64]{3,0,2,1:T(4,128)S(1)}, u32[]{:S(2)}, u32[]{:S(2)}) collective-permute-start(f32[3,1,26,64]{3,0,2,1:T(4,128)S(1)} %pad_maximum_fusion.8), channel_id=1, source_target_pairs={{0,2},{2,4},{4,6},{6,8},{8,10},{10,12},{12,14},{14,16},{16,18},{18... | collective-permute-start | bytes 59912 | tf_op jit(solution)/shard_map/ppermute | solution.py:33
  50.4 5.9 %collective-permute-start.8 = (f32[3,1,26,64]{3,0,2,1:T(4,128)S(1)}, f32[3,1,26,64]{3,0,2,1:T(4,128)S(1)}, u32[]{:S(2)}, u32[]{:S(2)}) collective-permute-start(f32[3,1,26,64]{3,0,2,1:T(4,128)S(1)} %pad_maximum_fusion.8), channel_id=1, source_target_pairs={{0,30},{2,0},{4,2},{6,4},{8,6},{10,8},{12,10},{14,12},{16,14},{18,... | collective-permute-start | bytes 59912 | tf_op jit(solution)/shard_map/ppermute | solution.py:33
  57.7 24.3 %collective-permute-start.7 = (f32[3,2,26,64]{3,0,2,1:T(4,128)}, f32[3,2,26,64]{3,0,2,1:T(4,128)S(1)}, u32[]{:S(2)}, u32[]{:S(2)}) collective-permute-start(f32[3,2,26,64]{3,0,2,1:T(4,128)} %get-tuple-element.76), channel_id=1, source_target_pairs={{0,4},{2,6},{4,8},{6,10},{8,12},{10,14},{12,16},{14,18},{16,20},{1... | collective-permute-start | bytes 119816 | tf_op jit(solution)/shard_map/ppermute | solution.py:33
  57.7 24.3 %collective-permute-start.9 = (f32[3,2,26,64]{3,0,2,1:T(4,128)S(1)}, f32[3,2,26,64]{3,0,2,1:T(4,128)S(1)}, u32[]{:S(2)}, u32[]{:S(2)}) collective-permute-start(f32[3,2,26,64]{3,0,2,1:T(4,128)S(1)} %get-tuple-element.77), channel_id=1, source_target_pairs={{0,28},{2,30},{4,0},{6,2},{8,4},{10,6},{12,8},{14,10},{16,12},{18,... | collective-permute-start | bytes 119816 | tf_op jit(solution)/shard_map/ppermute | solution.py:33
  63.1 22.8 %copy-start.2 = (f32[1,30,64,64]{3,2,1,0:T(8,128)S(1)}, f32[1,30,64,64]{3,2,1,0:T(8,128)}, u32[]{:S(2)}) copy-start(f32[1,30,64,64]{3,2,1,0:T(8,128)} %param.16) | copy-start | bytes 1474564
  82.8 11.7 %collective-permute-start.11 = (f32[3,4,26,64]{3,0,2,1:T(4,128)S(1)}, f32[3,4,26,64]{3,0,2,1:T(4,128)S(1)}, u32[]{:S(2)}, u32[]{:S(2)}) collective-permute-start(f32[3,4,26,64]{3,0,2,1:T(4,128)S(1)} %get-tuple-element.75), channel_id=1, source_target_pairs={{0,24},{2,26},{4,28},{6,30},{8,0},{10,2},{12,4},{14,6},{16,8},{18,... | collective-permute-start | bytes 239624 | tf_op jit(solution)/shard_map/ppermute | solution.py:33
  82.9 12.3 %collective-permute-start.10 = (f32[3,4,26,64]{3,0,2,1:T(4,128)S(1)}, f32[3,4,26,64]{3,0,2,1:T(4,128)S(1)}, u32[]{:S(2)}, u32[]{:S(2)}) collective-permute-start(f32[3,4,26,64]{3,0,2,1:T(4,128)S(1)} %get-tuple-element.74), channel_id=1, source_target_pairs={{0,8},{2,10},{4,12},{6,14},{8,16},{10,18},{12,20},{14,22},{16,24},... | collective-permute-start | bytes 239624 | tf_op jit(solution)/shard_map/ppermute | solution.py:33
  98.6 4.1 %collective-permute-start.3 = (f32[7,3,1,256]{3,0,2,1:T(8,128)S(1)}, f32[7,3,1,256]{3,0,2,1:T(8,128)S(1)}, u32[]{:S(2)}, u32[]{:S(2)}) collective-permute-start(f32[7,3,1,256]{3,0,2,1:T(8,128)S(1)} %get-tuple-element.32), channel_id=1, source_target_pairs={{1,0},{0,1},{3,2},{2,3},{5,4},{4,5},{7,6},{6,7},{9,8},{8,9},{11,10... | collective-permute-start | bytes 64520 | tf_op jit(solution)/shard_map/ppermute | solution.py:24
  100.6 3.9 %collective-permute-start.2 = (f32[7,3,1,256]{3,0,2,1:T(8,128)S(1)}, f32[7,3,1,256]{3,0,2,1:T(8,128)S(1)}, u32[]{:S(2)}, u32[]{:S(2)}) collective-permute-start(f32[7,3,1,256]{3,0,2,1:T(8,128)S(1)} %get-tuple-element.31), channel_id=1, source_target_pairs={{0,1},{1,0},{2,3},{3,2},{4,5},{5,4},{6,7},{7,6},{8,9},{9,8},{10,11... | collective-permute-start | bytes 64520 | tf_op jit(solution)/shard_map/ppermute | solution.py:22
  105.5 0.7 copy-start.10
  105.5 0.7 copy-start.11
  105.5 0.8 copy-start.12
  105.5 0.8 copy-start.13
  160.8 9.1 %copy-start.5 = (f32[3,1,24,256]{3,2,1,0:T(8,128)S(1)}, f32[3,1,24,256]{3,2,1,0:T(8,128)}, u32[]{:S(2)}) copy-start(f32[3,1,24,256]{3,2,1,0:T(8,128)} %param.10) | copy-start | bytes 221188
  160.8 9.1 %copy-start.9 = (f32[1,24,256]{2,1,0:T(8,128)S(1)}, f32[1,24,256]{2,1,0:T(8,128)}, u32[]{:S(2)}) copy-start(f32[1,24,256]{2,1,0:T(8,128)} %param.12) | copy-start | bytes 73732
where the time goes:
time: 191 us; the launch traced here: 190 us
  matrix products  97.9 us (51%)
  blocking collectives  25.5 us (13%)
  starting transfers between devices  25.3 us (13%)
  between operations  19.5 us (10%)
  waiting for transfers between devices  8.8 us (5%)
  local copies, waits for them, and re-layouts  6.93 us (4%)
  other arithmetic  6.05 us (3%)
    dot_general x9, matrix products, near_field(): jnp.einsum('alij,ralj->rali', kernel, source[4:], precision=HIGHEST_ACCUR...  82.1 us
    all_gather x1, blocking collectives, body(): every_sector = lax.all_gather(sector_coefs, 'blk', axis=1, tiled=True)  19.9 us
    ppermute x6, starting transfers between devices, passed_along(): return lax.ppermute(x, axis, [(i, (i + by) % count) for i in range(count)])  11.3 us
    ppermute x6, waiting for transfers between devices, passed_along(): return lax.ppermute(x, axis, [(i, (i + by) % count) for i in range(count)])  7.18 us
    dot_general x30, matrix products, add_sector(): jnp.einsum('skq,rslq->rslk', coupling, partner, precision=HIGHEST_ACCURACY)  7.17 us
    ppermute x3, starting transfers between devices, with_halo(): lax.ppermute(tail, axis, [(i, (i + 1) % count) for i in range(ends)])  7.16 us
    ppermute x3, starting transfers between devices, with_halo(): lax.ppermute(head, axis, [((i + 1) % count, i) for i in range(ends)])  6.83 us
    psum x1, blocking collectives, body(): sector_coefs = lax.psum(shared_portion, 'along')  5.63 us
  transfers between devices with their start and end apart: 12, of which 3 were waited for; matrix products, arithmetic and copies ran while one was open for 12% of the time, Pallas kernels for 0%

commit v1 on v0

--- a/solution.py
+++ b/solution.py
@@ -1,6 +1,8 @@
 import jax
 import jax.numpy as jnp
 from jax import lax
+from jax.experimental import pallas as pl
+from jax.experimental.pallas import tpu as pltpu
 from jax.sharding import PartitionSpec as P
 
 REACH = 6
@@ -33,27 +35,88 @@
     return lax.ppermute(x, axis, [(i, (i + by) % count) for i in range(count)])
 
 
+def split_in_two(x):
+    high = x.astype(jnp.bfloat16).astype(jnp.float32)
+    return high, x - high
+
+
+def near_kernel(cells_ref, out_ref, feature_ref, weight_ref):
+    leaves, _, size = out_ref.shape
+    row = lax.broadcasted_iota(jnp.int32, (8, size), 0)
+    log2e = 1.4426950408889634
+
+    def prepare(a):
+        def step(m, carry):
+            cell = cells_ref[a, m]
+            high, low = split_in_two(jnp.where(row < 3, cell, 0.0))
+            stacked = jnp.concatenate([high, low, high, low], 0)
+            feature_ref[a, m] = stacked.T.astype(jnp.bfloat16)
+            around = cell[0:1] + (a - 1.0)
+            radial = cell[2:3]
+            part = around * around + radial * radial
+            for b in range(3):
+                along = cell[1:2] + (b - 1.0)
+                factor = jnp.exp2((-SHARPNESS * log2e) * (part + along * along))
+                high, low = split_in_two(cell * factor)
+                weight_ref[a, m, b] = jnp.concatenate([high, low], 0).astype(jnp.bfloat16)
+            return carry
+
+        lax.fori_loop(0, leaves + 2, step, 0)
+
+    for a in range(3):
+        prepare(a)
+
+    def leaf(m, carry):
+        cell = cells_ref[1, m + 1]
+        high, low = split_in_two(jnp.where(row < 3, cell * (2 * SHARPNESS * log2e), 0.0))
+        target = jnp.concatenate([high, high, low, low], 0).astype(jnp.bfloat16)
+        x0, x1, x2 = cell[0:1], cell[1:2], cell[2:3]
+        base = (
+            KERNEL_SCALE
+            * cell[6:7]
+            * jnp.exp2((-SHARPNESS * log2e) * (x0 * x0 + x1 * x1 + x2 * x2))
+        )
+        total = jnp.zeros((8, size), jnp.float32)
+        for a in range(3):
+            for b in range(3):
+                power = jnp.dot(
+                    feature_ref[a, m + b], target, preferred_element_type=jnp.float32
+                )
+                tile = jnp.exp2(power)
+                tile_high = tile.astype(jnp.bfloat16)
+                tile_low = (tile - tile_high.astype(jnp.float32)).astype(jnp.bfloat16)
+                weight = weight_ref[a, m + b, b]
+                got = jnp.dot(weight, tile_high, preferred_element_type=jnp.float32) + jnp.dot(
+                    weight, tile_low, preferred_element_type=jnp.float32
+                )
+                factor = base * jnp.exp2(
+                    (2 * SHARPNESS * log2e) * ((a - 1.0) * x0 + (b - 1.0) * x1)
+                )
+                total = total + factor * (got[:8] + got[8:])
+        out_ref[m] = total
+        return carry
+
+    lax.fori_loop(0, leaves, leaf, 0)
+
+
 def near_field(padded):
-    leaves = padded.shape[2] - 2
-    center = padded[:, 1:2, 1 : 1 + leaves]
-    result = jnp.zeros((3, 1, leaves, padded.shape[3]), jnp.float32)
-    for around in (-1, 0, 1):
-        for along_step in (-1, 0, 1):
-            source = padded[:, 1 + around : 2 + around, 1 + along_step : 1 + along_step + leaves]
-            gap_around = around + source[0][..., None, :] - center[0][..., :, None]
-            gap_along = along_step + source[1][..., None, :] - center[1][..., :, None]
-            gap_radial = source[2][..., None, :] - center[2][..., :, None]
-            squared = gap_around * gap_around + gap_along * gap_along + gap_radial * gap_radial
-            kernel = (
-                KERNEL_SCALE
-                * center[3][..., :, None]
-                * source[3][..., None, :]
-                * jnp.exp(-SHARPNESS * squared)
-            )
-            result = result + jnp.einsum(
-                "alij,ralj->rali", kernel, source[4:], precision=HIGHEST_ACCURACY
-            )
-    return result
+    leaves = padded.shape[1] - 2
+    size = padded.shape[3]
+    tiles = 9 * leaves * size * size
+    return pl.pallas_call(
+        near_kernel,
+        out_shape=jax.ShapeDtypeStruct((leaves, 8, size), jnp.float32),
+        in_specs=[pl.BlockSpec(memory_space=pltpu.VMEM)],
+        out_specs=pl.BlockSpec(memory_space=pltpu.VMEM),
+        scratch_shapes=[
+            pltpu.VMEM((3, leaves + 2, size, 32), jnp.bfloat16),
+            pltpu.VMEM((3, leaves + 2, 3, 16, size), jnp.bfloat16),
+        ],
+        compiler_params=pltpu.CompilerParams(vmem_limit_bytes=40 * 1024 * 1024),
+        cost_estimate=pl.CostEstimate(
+            flops=100 * tiles, bytes_accessed=16 * padded.size, transcendentals=tiles
+        ),
+    )(padded)
 
 
 def slot_number(around, along_step, reach):
@@ -86,14 +149,22 @@
     top_coupling,
     top_admissible,
 ):
-    stacked = jnp.concatenate([offsets, stiffness[None], values], 0)
-    padded = with_halo(stacked, (("blk", 1), ("along", 2)), 1, True)
+    cells = jnp.concatenate(
+        [
+            offsets - 0.5,
+            stiffness[None] * values,
+            stiffness[None],
+            jnp.zeros_like(stiffness)[None],
+        ],
+        0,
+    ).transpose(1, 2, 0, 3)
+    padded = with_halo(cells, (("blk", 0), ("along", 1)), 1, True)
     at_start = lax.axis_index("along") == 0
     at_finish = lax.axis_index("along") == lax.axis_size("along") - 1
-    lower_rim = jnp.where(at_start, 0.0, padded[:, :, :1])
-    upper_rim = jnp.where(at_finish, 0.0, padded[:, :, -1:])
-    padded = jnp.concatenate([lower_rim, padded[:, :, 1:-1], upper_rim], 2)
-    near = near_field(padded)
+    lower_rim = jnp.where(at_start, 0.0, padded[:, :1])
+    upper_rim = jnp.where(at_finish, 0.0, padded[:, -1:])
+    padded = jnp.concatenate([lower_rim, padded[:, 1:-1], upper_rim], 1)
+    near = near_field(padded)[:, 3:6].transpose(1, 0, 2)[:, None]
     coefs = jnp.einsum("slki,rsli->rslk", leaf_basis, values, precision=HIGHEST_ACCURACY)
     rimmed = with_halo(coefs, (("along", 2),), 1, False)
     far_leaf = jnp.zeros(coefs.shape, jnp.float32)

time: 191 us -> 131 us (0.69)
  matrix products: 97.9 us -> 16.9 us
  Pallas kernels: 0 us -> 29.9 us
  other arithmetic: 6.05 us -> 2.06 us
  local copies, waits for them, and re-layouts: 6.93 us -> 3.27 us
    dot_general x9 -> x0, matrix products: 82.1 us -> none  [near_field(): jnp.einsum('alij,ralj->rali', kernel, source[4:], precision=HIGHEST_ACCUR...]
    pallas_call x0 -> x1, Pallas kernels: none -> 29.9 us  [near_field(): pl.pallas_call(near_kernel, out_shape=jax.ShapeDtypeStruct((leaves, 8, si...]
    unnamed x46 -> x14, local copies, waits for them, and re-layouts: 2.66 us -> 0.03 us
    ppermute x3, starting transfers between devices: 7.16 us -> 4.56 us  [with_halo(): lax.ppermute(tail, axis, [(i, (i + 1) % count) for i in range(ends)])]
  transfers between devices with their start and end apart: 12 -> 12, of which waited for: 3 -> 4; matrix products, arithmetic and copies ran while one was open for 12% -> 14% of each run, Pallas kernels for 0% -> 0%
where the time goes in v1:
time: 131 us; the launch traced here: 130 us
  Pallas kernels  29.9 us (23%)
  blocking collectives  24.5 us (19%)
  starting transfers between devices  24.3 us (19%)
  between operations  19.1 us (15%)
  matrix products  16.9 us (13%)
  waiting for transfers between devices  9.73 us (7%)
  local copies, waits for them, and re-layouts  3.27 us (2%)
  other arithmetic  2.06 us (2%)
    pallas_call x1, Pallas kernels, near_field(): pl.pallas_call(near_kernel, out_shape=jax.ShapeDtypeStruct((leaves, 8, si...  29.9 us
    all_gather x1, blocking collectives, body(): every_sector = lax.all_gather(sector_coefs, 'blk', axis=1, tiled=True)  19 us
    ppermute x6, starting transfers between devices, passed_along(): return lax.ppermute(x, axis, [(i, (i + by) % count) for i in range(count)])  11.3 us
    dot_general x30, matrix products, add_sector(): jnp.einsum('skq,rslq->rslk', coupling, partner, precision=HIGHEST_ACCURACY)  8.75 us
    ppermute x3, starting transfers between devices, with_halo(): lax.ppermute(head, axis, [((i + 1) % count, i) for i in range(ends)])  8.44 us
    ppermute x6, waiting for transfers between devices, passed_along(): return lax.ppermute(x, axis, [(i, (i + by) % count) for i in range(count)])  5.94 us
    psum x1, blocking collectives, body(): sector_coefs = lax.psum(shared_portion, 'along')  5.53 us
    ppermute x3, starting transfers between devices, with_halo(): lax.ppermute(tail, axis, [(i, (i + 1) % count) for i in range(ends)])  4.56 us
  transfers between devices with their start and end apart: 12, of which 4 were waited for; matrix products, arithmetic and copies ran while one was open for 14% of the time, Pallas kernels for 0%

profile of v1, /device:TPU:0, one launch (start us, length us, event | category | flops | bytes accessed | tf_op | source)
XLA Modules:
  0.0 129.8 jit_solution(2799412166668403476)
XLA Ops:
  0.0 0.9 broadcast_in_dim.10
  1.0 1.0 copy_multiply_fusion
  2.1 0.5 collective-permute-start
  2.7 5.0 %collective-permute-start.1 = (f32[1,24,8,256]{3,2,1,0:T(8,128)S(1)}, f32[1,24,8,256]{3,2,1,0:T(8,128)S(1)}, u32[]{:S(2)}, u32[]{:S(2)}) collective-permute-start(f32[1,24,8,256]{3,2,1,0:T(8,128)S(1)} %maximum_bitcast_fusion), channel_id=1, source_target_pairs={{2,0},{4,2},{6,4},{8,6},{10,8},{12,10},{14,12},{16,14},{18,16},{20... | collective-permute-start | bytes 589832 | tf_op jit(solution)/shard_map/ppermute | solution.py:26
  7.7 2.3 %fusion.2 = f32[24,3,64]{2,1,0:T(4,128)S(1)} fusion(f32[1,24,64,256]{3,2,1,0:T(8,128)S(1)} %copy-done, f32[3,24,256]{2,1,0:T(8,128)} %bitcast.304), kind=kOutput, calls=%fused_computation.2 | convolution fusion | flops 14155776 | bytes 1665024 | tf_op jit(solution)/shard_map/slki,rsli->rslk/dot_general | solution.py:168
  10.0 3.9 %collective-permute-start.4 = (f32[3,1,1,64]{3,0,2,1:T(4,128)S(1)}, f32[3,1,1,64]{3,0,2,1:T(4,128)S(1)}, u32[]{:S(2)}, u32[]{:S(2)}) collective-permute-start(f32[3,1,1,64]{3,0,2,1:T(4,128)S(1)} %get-tuple-element.41), channel_id=1, source_target_pairs={{0,1},{2,3},{4,5},{6,7},{8,9},{10,11},{12,13},{14,15},{16,17},{18,... | collective-permute-start | bytes 2312 | tf_op jit(solution)/shard_map/ppermute | solution.py:24
  13.9 1.3 collective-permute-start.5
  15.2 0.5 convolution_bitcast_fusion.3
  15.9 5.5 %psum.7 = f32[3,1,64]{2,0,1:T(4,128)S(1)} all-reduce(f32[3,1,64]{2,0,1:T(4,128)S(1)} %convolution_bitcast_fusion.2), channel_id=1, replica_groups=mesh['blk'=16,'along'=2] {'along'}, use_global_device_ids=true, to_apply=%region_0.1 | all-reduce | flops 192 | bytes 1536 | tf_op jit(solution)/shard_map/psum | solution.py:205
  21.4 19.0 %all_gather.3 = f32[3,16,64]{2,0,1:T(4,128)S(1)} all-gather(f32[3,1,64]{2,0,1:T(4,128)S(1)} %psum.7), channel_id=1, replica_groups=mesh['blk'=16,'along'=2] {'blk'}, dimensions={1}, use_global_device_ids=true | all-gather | bytes 13056 | tf_op jit(solution)/shard_map/all_gather | solution.py:206
  40.4 1.6 %convolution_bitcast_fusion = f32[3,64]{1,0:T(4,128)S(1)} fusion(f32[3,16,64]{2,0,1:T(4,128)S(1)} %all_gather.3, f32[1,16,64,64]{3,2,1,0:T(8,128)} %param.18, f32[16]{0:T(128)S(1)} %and_select_fusion), kind=kOutput, calls=%fused_computation.36 | convolution fusion | flops 2424832 | bytes 275264 | tf_op jit(solution)/shard_map/stkq,rtq->rsk/dot_general | solution.py:212
  42.2 2.6 %fusion.39 = f32[3,24,64]{2,0,1:T(4,128)} fusion(f32[3,64,1]{1,0,2:T(4,128)S(1)} %convolution_bitcast_fusion.1, f32[1,24,64,64]{3,2,1,0:T(8,128)S(1)} %copy-done.1), kind=kOutput, calls=%fused_computation.40 | convolution fusion | flops 3538944 | bytes 412416 | tf_op jit(solution)/shard_map/slqk,rsk->rslq/dot_general | solution.py:221
  44.8 0.4 collective-permute-start.6
  45.2 4.1 %collective-permute-start.8 = (f32[3,1,26,64]{3,0,2,1:T(4,128)S(1)}, f32[3,1,26,64]{3,0,2,1:T(4,128)S(1)}, u32[]{:S(2)}, u32[]{:S(2)}) collective-permute-start(f32[3,1,26,64]{3,0,2,1:T(4,128)S(1)} %pad_maximum_fusion.7), channel_id=1, source_target_pairs={{0,30},{2,0},{4,2},{6,4},{8,6},{10,8},{12,10},{14,12},{16,14},{18,... | collective-permute-start | bytes 59912 | tf_op jit(solution)/shard_map/ppermute | solution.py:35
  49.3 0.7 fusion.231
  50.1 1.1 collective-permute-done.6
  51.2 0.7 pad_maximum_fusion.4
  51.9 4.7 %collective-permute-start.9 = (f32[3,2,26,64]{3,0,2,1:T(4,128)}, f32[3,2,26,64]{3,0,2,1:T(4,128)S(1)}, u32[]{:S(2)}, u32[]{:S(2)}) collective-permute-start(f32[3,2,26,64]{3,0,2,1:T(4,128)} %get-tuple-element.40), channel_id=1, source_target_pairs={{0,28},{2,30},{4,0},{6,2},{8,4},{10,6},{12,8},{14,10},{16,12},{18,... | collective-permute-start | bytes 119816 | tf_op jit(solution)/shard_map/ppermute | solution.py:35
  56.6 0.7 fusion.232
  76.2 2.0 %collective-permute-start.10 = (f32[3,4,26,64]{3,0,2,1:T(4,128)S(1)}, f32[3,4,26,64]{3,0,2,1:T(4,128)S(1)}, u32[]{:S(2)}, u32[]{:S(2)}) collective-permute-start(f32[3,4,26,64]{3,0,2,1:T(4,128)S(1)} %get-tuple-element.37), channel_id=1, source_target_pairs={{0,8},{2,10},{4,12},{6,14},{8,16},{10,18},{12,20},{14,22},{16,24},... | collective-permute-start | bytes 239624 | tf_op jit(solution)/shard_map/ppermute | solution.py:35
  78.2 1.0 fusion.84
  79.2 1.0 fusion.86
  80.2 1.0 fusion.100
  81.7 0.2 fusion.88
  83.0 4.8 %collective-permute-done.11 = f32[3,4,26,64]{3,0,2,1:T(4,128)S(1)} collective-permute-done((f32[3,4,26,64]{3,0,2,1:T(4,128)S(1)}, f32[3,4,26,64]{3,0,2,1:T(4,128)S(1)}, u32[]{:S(2)}, u32[]{:S(2)}) %collective-permute-start.11) | collective-permute-done | bytes 79904 | tf_op jit(solution)/shard_map/ppermute | solution.py:35
  92.0 2.1 %collective-permute-start.3 = (f32[3,1,8,256]{3,2,1,0:T(8,128)S(1)}, f32[3,1,8,256]{3,2,1,0:T(8,128)S(1)}, u32[]{:S(2)}, u32[]{:S(2)}) collective-permute-start(f32[3,1,8,256]{3,2,1,0:T(8,128)S(1)} %get-tuple-element.6), channel_id=1, source_target_pairs={{1,0},{0,1},{3,2},{2,3},{5,4},{4,5},{7,6},{6,7},{9,8},{8,9},{11,10... | collective-permute-start | bytes 73736 | tf_op jit(solution)/shard_map/ppermute | solution.py:26
  94.1 0.3 fusion.38
  94.5 1.5 %collective-permute-done.3 = f32[3,1,8,256]{3,2,1,0:T(8,128)S(1)} collective-permute-done((f32[3,1,8,256]{3,2,1,0:T(8,128)S(1)}, f32[3,1,8,256]{3,2,1,0:T(8,128)S(1)}, u32[]{:S(2)}, u32[]{:S(2)}) %collective-permute-start.3) | collective-permute-done | bytes 24608 | tf_op jit(solution)/shard_map/ppermute | solution.py:26
  96.0 2.3 %collective-permute-done.2 = f32[3,1,8,256]{3,2,1,0:T(8,128)S(1)} collective-permute-done((f32[3,1,8,256]{3,2,1,0:T(8,128)S(1)}, f32[3,1,8,256]{3,2,1,0:T(8,128)S(1)}, u32[]{:S(2)}, u32[]{:S(2)}) %collective-permute-start.2) | collective-permute-done | bytes 24608 | tf_op jit(solution)/shard_map/ppermute | solution.py:24
  98.3 29.9 %shard_map.100 = f32[24,8,256]{2,1,0:T(8,128)S(1)} custom-call(f32[3,26,8,256]{3,2,1,0:T(8,128)S(1)} %pad_maximum_fusion.cells_ref), custom_call_target="tpu_custom_call" | custom-call | flops 1415577600 | bytes 2555904 | tf_op jit(solution)/shard_map/pallas_call | solution.py:106
  128.3 0.9 fusion.7
  129.1 0.7 copy.55
  (66 shorter events, 6.4 us)
Async XLA Ops:
  0.0 7.7 %copy-start = (f32[1,24,64,256]{3,2,1,0:T(8,128)S(1)}, f32[1,24,64,256]{3,2,1,0:T(8,128)}, u32[]{:S(2)}) copy-start(f32[1,24,64,256]{3,2,1,0:T(8,128)} %param.13) | copy-start | bytes 4718596
  0.0 15.2 %copy-start.1 = (f32[1,24,64,64]{3,2,1,0:T(8,128)S(1)}, f32[1,24,64,64]{3,2,1,0:T(8,128)}, u32[]{:S(2)}) copy-start(f32[1,24,64,64]{3,2,1,0:T(8,128)} %param.14) | copy-start | bytes 1179652
  2.0 13.7 %copy-start.5 = (f32[1,1,64,64]{3,2,1,0:T(8,128)S(1)}, f32[1,1,64,64]{3,2,1,0:T(8,128)}, u32[]{:S(2)}) copy-start(f32[1,1,64,64]{3,2,1,0:T(8,128)} %param.15) | copy-start | bytes 49156
  2.0 38.4 %copy-start.6 = (s32[1,16]{1,0:T(1,128)S(1)}, s32[1,16]{1,0:T(1,128)}, u32[]{:S(2)}) copy-start(s32[1,16]{1,0:T(1,128)} %param.19) | copy-start | bytes 196
  2.1 89.8 %collective-permute-start = (f32[1,24,8,256]{3,2,1,0:T(8,128)S(1)}, f32[1,24,8,256]{3,2,1,0:T(8,128)S(1)}, u32[]{:S(2)}, u32[]{:S(2)}) collective-permute-start(f32[1,24,8,256]{3,2,1,0:T(8,128)S(1)} %maximum_bitcast_fusion), channel_id=1, source_target_pairs={{0,2},{2,4},{4,6},{6,8},{8,10},{10,12},{12,14},{14,16},{16,18},{18... | collective-permute-start | bytes 589832 | tf_op jit(solution)/shard_map/ppermute | solution.py:24
  2.7 89.3 %collective-permute-start.1 = (f32[1,24,8,256]{3,2,1,0:T(8,128)S(1)}, f32[1,24,8,256]{3,2,1,0:T(8,128)S(1)}, u32[]{:S(2)}, u32[]{:S(2)}) collective-permute-start(f32[1,24,8,256]{3,2,1,0:T(8,128)S(1)} %maximum_bitcast_fusion), channel_id=1, source_target_pairs={{2,0},{4,2},{6,4},{8,6},{10,8},{12,10},{14,12},{16,14},{18,16},{20... | collective-permute-start | bytes 589832 | tf_op jit(solution)/shard_map/ppermute | solution.py:26
  10.0 39.4 %copy-start.3 = (s32[1,30]{1,0:T(1,128)S(1)}, s32[1,30]{1,0:T(1,128)}, u32[]{:S(2)}) copy-start(s32[1,30]{1,0:T(1,128)} %param.17) | copy-start | bytes 364
  10.0 34.8 %collective-permute-start.4 = (f32[3,1,1,64]{3,0,2,1:T(4,128)S(1)}, f32[3,1,1,64]{3,0,2,1:T(4,128)S(1)}, u32[]{:S(2)}, u32[]{:S(2)}) collective-permute-start(f32[3,1,1,64]{3,0,2,1:T(4,128)S(1)} %get-tuple-element.41), channel_id=1, source_target_pairs={{0,1},{2,3},{4,5},{6,7},{8,9},{10,11},{12,13},{14,15},{16,17},{18,... | collective-permute-start | bytes 2312 | tf_op jit(solution)/shard_map/ppermute | solution.py:24
  13.9 30.9 %collective-permute-start.5 = (f32[3,1,1,64]{3,0,2,1:T(4,128)S(1)}, f32[3,1,1,64]{3,0,2,1:T(4,128)S(1)}, u32[]{:S(2)}, u32[]{:S(2)}) collective-permute-start(f32[3,1,1,64]{3,0,2,1:T(4,128)S(1)} %get-tuple-element.42), channel_id=1, source_target_pairs={{1,0},{3,2},{5,4},{7,6},{9,8},{11,10},{13,12},{15,14},{17,16},{19,... | collective-permute-start | bytes 2312 | tf_op jit(solution)/shard_map/ppermute | solution.py:26
  44.8 36.4 %copy-start.2 = (f32[1,30,64,64]{3,2,1,0:T(8,128)S(1)}, f32[1,30,64,64]{3,2,1,0:T(8,128)}, u32[]{:S(2)}) copy-start(f32[1,30,64,64]{3,2,1,0:T(8,128)} %param.16) | copy-start | bytes 1474564
  44.8 6.3 %collective-permute-start.6 = (f32[3,1,26,64]{3,0,2,1:T(4,128)S(1)}, f32[3,1,26,64]{3,0,2,1:T(4,128)S(1)}, u32[]{:S(2)}, u32[]{:S(2)}) collective-permute-start(f32[3,1,26,64]{3,0,2,1:T(4,128)S(1)} %pad_maximum_fusion.7), channel_id=1, source_target_pairs={{0,2},{2,4},{4,6},{6,8},{8,10},{10,12},{12,14},{14,16},{16,18},{18... | collective-permute-start | bytes 59912 | tf_op jit(solution)/shard_map/ppermute | solution.py:35
  45.2 5.9 %collective-permute-start.8 = (f32[3,1,26,64]{3,0,2,1:T(4,128)S(1)}, f32[3,1,26,64]{3,0,2,1:T(4,128)S(1)}, u32[]{:S(2)}, u32[]{:S(2)}) collective-permute-start(f32[3,1,26,64]{3,0,2,1:T(4,128)S(1)} %pad_maximum_fusion.7), channel_id=1, source_target_pairs={{0,30},{2,0},{4,2},{6,4},{8,6},{10,8},{12,10},{14,12},{16,14},{18,... | collective-permute-start | bytes 59912 | tf_op jit(solution)/shard_map/ppermute | solution.py:35
  51.9 24.1 %collective-permute-start.7 = (f32[3,2,26,64]{3,0,2,1:T(4,128)}, f32[3,2,26,64]{3,0,2,1:T(4,128)S(1)}, u32[]{:S(2)}, u32[]{:S(2)}) collective-permute-start(f32[3,2,26,64]{3,0,2,1:T(4,128)} %get-tuple-element.39), channel_id=1, source_target_pairs={{0,4},{2,6},{4,8},{6,10},{8,12},{10,14},{12,16},{14,18},{16,20},{1... | collective-permute-start | bytes 119816 | tf_op jit(solution)/shard_map/ppermute | solution.py:35
  51.9 24.1 %collective-permute-start.9 = (f32[3,2,26,64]{3,0,2,1:T(4,128)}, f32[3,2,26,64]{3,0,2,1:T(4,128)S(1)}, u32[]{:S(2)}, u32[]{:S(2)}) collective-permute-start(f32[3,2,26,64]{3,0,2,1:T(4,128)} %get-tuple-element.40), channel_id=1, source_target_pairs={{0,28},{2,30},{4,0},{6,2},{8,4},{10,6},{12,8},{14,10},{16,12},{18,... | collective-permute-start | bytes 119816 | tf_op jit(solution)/shard_map/ppermute | solution.py:35
  76.1 11.7 %collective-permute-start.11 = (f32[3,4,26,64]{3,0,2,1:T(4,128)S(1)}, f32[3,4,26,64]{3,0,2,1:T(4,128)S(1)}, u32[]{:S(2)}, u32[]{:S(2)}) collective-permute-start(f32[3,4,26,64]{3,0,2,1:T(4,128)S(1)} %get-tuple-element.38), channel_id=1, source_target_pairs={{0,24},{2,26},{4,28},{6,30},{8,0},{10,2},{12,4},{14,6},{16,8},{18,... | collective-permute-start | bytes 239624 | tf_op jit(solution)/shard_map/ppermute | solution.py:35
  76.2 11.9 %collective-permute-start.10 = (f32[3,4,26,64]{3,0,2,1:T(4,128)S(1)}, f32[3,4,26,64]{3,0,2,1:T(4,128)S(1)}, u32[]{:S(2)}, u32[]{:S(2)}) collective-permute-start(f32[3,4,26,64]{3,0,2,1:T(4,128)S(1)} %get-tuple-element.37), channel_id=1, source_target_pairs={{0,8},{2,10},{4,12},{6,14},{8,16},{10,18},{12,20},{14,22},{16,24},... | collective-permute-start | bytes 239624 | tf_op jit(solution)/shard_map/ppermute | solution.py:35
  88.1 6.0 %copy-start.4 = (f32[3,24,64]{2,0,1:T(4,128)S(1)}, f32[3,24,64]{2,0,1:T(4,128)}, u32[]{:S(2)}) copy-start(f32[3,24,64]{2,0,1:T(4,128)} %fusion.39) | copy-start | bytes 55300
  92.0 4.0 %collective-permute-start.3 = (f32[3,1,8,256]{3,2,1,0:T(8,128)S(1)}, f32[3,1,8,256]{3,2,1,0:T(8,128)S(1)}, u32[]{:S(2)}, u32[]{:S(2)}) collective-permute-start(f32[3,1,8,256]{3,2,1,0:T(8,128)S(1)} %get-tuple-element.6), channel_id=1, source_target_pairs={{1,0},{0,1},{3,2},{2,3},{5,4},{4,5},{7,6},{6,7},{9,8},{8,9},{11,10... | collective-permute-start | bytes 73736 | tf_op jit(solution)/shard_map/ppermute | solution.py:26
  94.4 3.9 %collective-permute-start.2 = (f32[3,1,8,256]{3,2,1,0:T(8,128)S(1)}, f32[3,1,8,256]{3,2,1,0:T(8,128)S(1)}, u32[]{:S(2)}, u32[]{:S(2)}) collective-permute-start(f32[3,1,8,256]{3,2,1,0:T(8,128)S(1)} %get-tuple-element.5), channel_id=1, source_target_pairs={{0,1},{1,0},{2,3},{3,2},{4,5},{5,4},{6,7},{7,6},{8,9},{9,8},{10,11... | collective-permute-start | bytes 73736 | tf_op jit(solution)/shard_map/ppermute | solution.py:24

commit v2 on v1

--- a/solution.py
+++ b/solution.py
@@ -11,28 +11,6 @@
 SHARPNESS = 2.0
 KERNEL_SCALE = 0.125
 HIGHEST_ACCURACY = lax.Precision.HIGHEST
-
-
-def with_halo(cells, sides, width, closed):
-    for axis, dim in sides:
-        count = lax.axis_size(axis)
-        ends = count if closed else count - 1
-        head = lax.slice_in_dim(cells, 0, width, axis=dim)
-        tail = lax.slice_in_dim(cells, cells.shape[dim] - width, cells.shape[dim], axis=dim)
-        cells = jnp.concatenate(
-            [
-                lax.ppermute(tail, axis, [(i, (i + 1) % count) for i in range(ends)]),
-                cells,
-                lax.ppermute(head, axis, [((i + 1) % count, i) for i in range(ends)]),
-            ],
-            axis=dim,
-        )
-    return cells
-
-
-def passed_along(x, axis, by):
-    count = lax.axis_size(axis)
-    return lax.ppermute(x, axis, [(i, (i + by) % count) for i in range(count)])
 
 
 def split_in_two(x):
@@ -119,22 +97,122 @@
     )(padded)
 
 
-def slot_number(around, along_step, reach):
-    block = around - 2 if around > 0 else reach - 1 + (-around - 2)
-    return 3 * block + along_step + 1
-
-
-def add_sector(total, held, around, leaf_coupling_matrices, leaf_admissible_mask):
-    leaves = total.shape[2]
-    for along_step in (-1, 0, 1):
-        slot = slot_number(around, along_step, REACH)
-        partner = held[:, :, 1 + along_step : 1 + along_step + leaves]
-        coupling = (
-            leaf_coupling_matrices[:, slot]
-            * leaf_admissible_mask[:, slot].astype(jnp.float32)[:, None, None]
+def far_offsets():
+    ahead = list(range(2, REACH + 1))
+    return ahead + [-step for step in ahead]
+
+
+def exchange_kernel(
+    cells_ref,
+    coefs_ref,
+    ends_ref,
+    share_ref,
+    padded_ref,
+    windows_ref,
+    rims_ref,
+    shares_ref,
+    send_sem,
+    recv_sem,
+    share_send_sem,
+    share_recv_sem,
+):
+    sectors, slabs = lax.axis_size("blk"), lax.axis_size("along")
+    sector, slab = lax.axis_index("blk"), lax.axis_index("along")
+    leaves = cells_ref.shape[0]
+    copies = []
+
+    def send(source, target, around, along):
+        k = len(copies)
+        copy = pltpu.make_async_remote_copy(
+            src_ref=source,
+            dst_ref=target,
+            send_sem=send_sem.at[k],
+            recv_sem=recv_sem.at[k],
+            device_id={
+                "blk": lax.rem(sector + around + sectors, sectors),
+                "along": lax.rem(slab + along + slabs, slabs),
+            },
+            device_id_type=pl.DeviceIdType.MESH,
         )
-        total = total + jnp.einsum("skq,rslq->rslk", coupling, partner, precision=HIGHEST_ACCURACY)
-    return total
+        copy.start()
+        copies.append(copy)
+
+    distant = sectors - 2 * REACH - 1
+
+    def share_copy(k, row, column):
+        return pltpu.make_async_remote_copy(
+            src_ref=share_ref,
+            dst_ref=shares_ref.at[row, column],
+            send_sem=share_send_sem.at[k],
+            recv_sem=share_recv_sem.at[k // slabs * slabs + column],
+            device_id={
+                "blk": lax.rem(sector + REACH + 1 + k // slabs, sectors),
+                "along": lax.rem(k, slabs),
+            },
+            device_id_type=pl.DeviceIdType.MESH,
+        )
+
+    def share_start(k, carry):
+        share_copy(k, sector, slab).start()
+        return carry
+
+    def share_wait(k, carry):
+        came = lax.rem(sector + sectors - REACH - 1 - k // slabs, sectors)
+        share_copy(k, sector, slab).wait_send()
+        share_copy(k, came, lax.rem(k, slabs)).wait_recv()
+        return carry
+
+    lax.fori_loop(0, distant * slabs, share_start, 0)
+    for around in (-1, 1):
+        send(cells_ref, padded_ref.at[1 - around, pl.ds(1, leaves)], around, 0)
+    for around in (-1, 0, 1):
+        send(cells_ref.at[leaves - 1], padded_ref.at[1 - around, 0], around, 1)
+        send(cells_ref.at[0], padded_ref.at[1 - around, leaves + 1], around, -1)
+    for q, around in enumerate(far_offsets()):
+        send(coefs_ref, windows_ref.at[q], -around, 0)
+        send(ends_ref.at[1], rims_ref.at[q, 0], -around, 1)
+        send(ends_ref.at[0], rims_ref.at[q, 1], -around, -1)
+    padded_ref[1, pl.ds(1, leaves)] = cells_ref[...]
+    for copy in copies:
+        copy.wait()
+    lax.fori_loop(0, distant * slabs, share_wait, 0)
+
+    @pl.when(slab == 0)
+    def _():
+        padded_ref[:, 0] = jnp.zeros_like(padded_ref[:, 0])
+        rims_ref[:, 0] = jnp.zeros_like(rims_ref[:, 0])
+
+    @pl.when(slab == slabs - 1)
+    def _():
+        padded_ref[:, leaves + 1] = jnp.zeros_like(padded_ref[:, 0])
+        rims_ref[:, 1] = jnp.zeros_like(rims_ref[:, 0])
+
+
+def exchange(cells, coefs, ends, share):
+    sectors, slabs = lax.axis_size("blk"), lax.axis_size("along")
+    leaves, _, size = cells.shape
+    far = 2 * (REACH - 1)
+    links = 8 + 3 * far
+    pairs = (sectors - 2 * REACH - 1) * slabs
+    vmem = pl.BlockSpec(memory_space=pltpu.VMEM)
+    return pl.pallas_call(
+        exchange_kernel,
+        out_shape=(
+            jax.ShapeDtypeStruct((3, leaves + 2, 8, size), jnp.float32),
+            jax.ShapeDtypeStruct((far, *coefs.shape), jnp.float32),
+            jax.ShapeDtypeStruct((far, *ends.shape), jnp.float32),
+            jax.ShapeDtypeStruct((sectors, slabs, *share.shape), jnp.float32),
+        ),
+        in_specs=[vmem] * 4,
+        out_specs=(vmem,) * 4,
+        scratch_shapes=[
+            pltpu.SemaphoreType.DMA((links,)),
+            pltpu.SemaphoreType.DMA((links,)),
+            pltpu.SemaphoreType.DMA((pairs,)),
+            pltpu.SemaphoreType.DMA((pairs,)),
+        ],
+        compiler_params=pltpu.CompilerParams(has_side_effects=True),
+    )(cells, coefs, ends, share)
 
 
 def body(
@@ -158,41 +236,7 @@
         ],
         0,
     ).transpose(1, 2, 0, 3)
-    padded = with_halo(cells, (("blk", 0), ("along", 1)), 1, True)
-    at_start = lax.axis_index("along") == 0
-    at_finish = lax.axis_index("along") == lax.axis_size("along") - 1
-    lower_rim = jnp.where(at_start, 0.0, padded[:, :1])
-    upper_rim = jnp.where(at_finish, 0.0, padded[:, -1:])
-    padded = jnp.concatenate([lower_rim, padded[:, 1:-1], upper_rim], 1)
-    near = near_field(padded)[:, 3:6].transpose(1, 0, 2)[:, None]
     coefs = jnp.einsum("slki,rsli->rslk", leaf_basis, values, precision=HIGHEST_ACCURACY)
-    rimmed = with_halo(coefs, (("along", 2),), 1, False)
-    far_leaf = jnp.zeros(coefs.shape, jnp.float32)
-    sectors = lax.axis_size("blk")
-    lower_window = rimmed
-    upper_window = rimmed
-    breadth = 1
-    while breadth <= REACH:
-        lower_came = passed_along(lower_window, "blk", breadth)
-        upper_came = passed_along(upper_window, "blk", -breadth)
-        lower_window = jnp.concatenate([lower_window, lower_came], 1)
-        upper_window = jnp.concatenate([upper_window, upper_came], 1)
-        breadth = 2 * breadth
-    for distance in range(2, REACH + 1):
-        far_leaf = add_sector(
-            far_leaf,
-            lower_window[:, distance : distance + 1],
-            -distance,
-            leaf_coupling_matrices,
-            leaf_admissible_mask,
-        )
-        far_leaf = add_sector(
-            far_leaf,
-            upper_window[:, distance : distance + 1],
-            distance,
-            leaf_coupling_matrices,
-            leaf_admissible_mask,
-        )
     slab_coefficient_rows = jnp.einsum(
         "slqk,rslq->rsk", transfer, coefs, precision=HIGHEST_ACCURACY
     )
@@ -202,13 +246,38 @@
         slab_coefficient_rows,
         precision=HIGHEST_ACCURACY,
     )
-    sector_coefs = lax.psum(shared_portion, "along")
-    every_sector = lax.all_gather(sector_coefs, "blk", axis=1, tiled=True)
+    by_leaf = coefs[:, 0].transpose(1, 0, 2)
+    leaves, count, rank = by_leaf.shape
+    width = -(-count * rank // 128) * 128
+    lanes = -(-rank // 128) * 128
+    flat = by_leaf.reshape(leaves, count * rank)
+    ends = jnp.stack([by_leaf[0], by_leaf[-1]])
+    padded, windows, rims, shares = exchange(
+        cells[0],
+        jnp.pad(flat, ((0, 0), (0, width - count * rank))),
+        jnp.pad(ends, ((0, 0), (0, 8 - count), (0, lanes - rank))),
+        jnp.pad(shared_portion[:, 0], ((0, 8 - count), (0, lanes - rank))),
+    )
+    near = near_field(padded)[:, 3:6].transpose(1, 0, 2)[:, None]
+    far = windows.shape[0]
+    windows = windows[:, :, : count * rank].reshape(far, leaves, count, rank)
+    rims = rims[:, :, :count, :rank]
+    windows = jnp.concatenate([rims[:, :1], windows, rims[:, 1:]], 1)
+    partners = jnp.stack([windows[:, b : b + leaves] for b in range(3)], 1)
+    coupling = (
+        leaf_coupling_matrices[0] * leaf_admissible_mask[0].astype(jnp.float32)[:, None, None]
+    ).reshape(far, 3, rank, rank)
+    far_leaf = jnp.einsum(
+        "qbkz,qblrz->rlk", coupling, partners, precision=HIGHEST_ACCURACY
+    )[:, None]
+    sectors = lax.axis_size("blk")
     sector = lax.axis_index("blk")
     others = jnp.arange(sectors, dtype=jnp.int32)
     apart = (others - sector) % sectors
-    distant = jnp.logical_and(apart > REACH, apart < sectors - REACH).astype(jnp.float32)
-    allowed = top_admissible[0].astype(jnp.float32) * distant
+    distant = jnp.logical_and(apart > REACH, apart < sectors - REACH)
+    allowed = jnp.where(distant, top_admissible[0].astype(jnp.float32), 0.0)
+    shares = jnp.where(distant[:, None, None, None], shares, 0.0)
+    every_sector = shares.sum(1)[:, :count, :rank].transpose(1, 0, 2)
     sector_local_coefs = jnp.einsum(
         "stkq,rtq->rsk",
         top_coupling * allowed[None, :, None, None],

time: 131 us -> 72.7 us (0.55)
  Pallas kernels: 29.9 us -> 55.7 us
  blocking collectives: 24.5 us -> 0 us
  starting transfers between devices: 24.3 us -> 0 us
  between operations: 19.1 us -> 0.18 us
  waiting for transfers between devices: 9.73 us -> 0 us
  matrix products: 16.9 us -> 7.66 us
  local copies, waits for them, and re-layouts: 3.27 us -> 5.65 us
    pallas_call x0 -> x1, Pallas kernels: none -> 25.8 us  [exchange(): pl.pallas_call(exchange_kernel, out_shape=(jax.ShapeDtypeStruct((3, leave...]
    ppermute x12 -> x0, starting transfers between devices: 24.3 us -> none  [the longest x6 11.3 us: passed_along(): return lax.ppermute(x, axis, [(i, (i + by) % count) for i in range(count)])]
    all_gather x1 -> x0, blocking collectives: 19 us -> none  [body(): every_sector = lax.all_gather(sector_coefs, 'blk', axis=1, tiled=True)]
    ppermute x12 -> x0, waiting for transfers between devices: 9.73 us -> none  [the longest x6 5.94 us: passed_along(): return lax.ppermute(x, axis, [(i, (i + by) % count) for i in range(count)])]
    dot_general x30 -> x1, matrix products: 8.75 us -> 1.18 us  [body(): jnp.einsum('qbkz,qblrz->rlk', coupling, partners, precision=HIGHEST_ACCUR...]
    psum x1 -> x0, blocking collectives: 5.53 us -> none  [body(): sector_coefs = lax.psum(shared_portion, 'along')]
    unnamed x14 -> x24, local copies, waits for them, and re-layouts: 0.03 us -> 2.18 us
    slice x3 -> x4, local copies, waits for them, and re-layouts: 1.41 us -> 0.04 us  [the longest x3 0.04 us: body(): windows = jnp.concatenate([rims[:, :1], windows, rims[:, 1:]], 1)]
  transfers between devices with their start and end apart: 12 -> 0, of which waited for: 4 -> 0; matrix products, arithmetic and copies ran while one was open for 14% -> 0% of each run, Pallas kernels for 0% -> 0%
where the time goes in v2:
time: 72.7 us; the launch traced here: 72.3 us
  Pallas kernels  55.7 us (77%)
  matrix products  7.66 us (11%)
  local copies, waits for them, and re-layouts  5.65 us (8%)
  other arithmetic  3.14 us (4%)
    pallas_call x1, Pallas kernels, near_field(): pl.pallas_call(near_kernel, out_shape=jax.ShapeDtypeStruct((leaves, 8, si...  29.9 us
    pallas_call x1, Pallas kernels, exchange(): pl.pallas_call(exchange_kernel, out_shape=(jax.ShapeDtypeStruct((3, leave...  25.8 us
    dot_general x1, matrix products, body(): jnp.einsum('slki,rsli->rslk', leaf_basis, values, precision=HIGHEST_ACCUR...  2.26 us
    unnamed x24, local copies, waits for them, and re-layouts  2.18 us
    dot_general x1, matrix products, body(): jnp.einsum('slqk,rsk->rslq', transfer, slab_local_coefs, precision=HIGHES...  1.94 us

profile of v2, /device:TPU:0, one launch (start us, length us, event | category | flops | bytes accessed | tf_op | source)
XLA Modules:
  0.0 72.3 jit_solution(9887677796753854466)
XLA Ops:
  0.0 0.0 copy-start.6
  0.0 0.8 %convert_reduce_fusion = f32[30]{0:T(128)S(1)} fusion(s32[1,30]{1,0:T(1,128)} %param.17), kind=kLoop, calls=%fused_computation.50 | loop fusion | flops 30 | bytes 240 | tf_op jit(solution)/shard_map/convert_element_type | solution.py:268
  0.9 0.7 bitcast_select_fusion
  1.5 0.1 pad.27.clone
  1.6 0.1 convert_element_type.27
  1.7 0.1 copy.28
  1.8 0.8 %broadcast_in_dim.27 = f32[1,1,24,256]{3,0,2,1:T(1,128)S(1)} reshape(f32[1,24,256]{2,1,0:T(8,128)} %param.12) | data formatting | bytes 49152 | tf_op jit(solution)/shard_map/broadcast_in_dim | solution.py:233
  2.6 2.3 %fusion.2 = f32[24,3,64]{2,1,0:T(4,128)S(1)} fusion(f32[1,24,64,256]{3,2,1,0:T(8,128)S(1)} %copy-done, f32[3,24,256]{2,1,0:T(8,128)} %bitcast.88), kind=kOutput, calls=%fused_computation.2 | convolution fusion | flops 14155776 | bytes 1665024 | tf_op jit(solution)/shard_map/slki,rsli->rslk/dot_general | solution.py:239
  4.8 0.5 convolution_bitcast_fusion.3
  5.4 0.1 fusion.30
  5.5 0.6 pad.14.share_ref
  6.1 0.1 reshape.109
  6.2 0.6 pad.12.coefs_ref
  6.8 0.6 select_maximum_fusion.ends_ref
  7.4 0.1 copy_multiply_fusion.2
  7.5 0.8 %maximum_bitcast_fusion.cells_ref = f32[24,8,256]{2,1,0:T(8,128)} fusion(f32[1,1,24,256]{3,0,2,1:T(1,128)S(1)} %broadcast_in_dim.27, f32[3,1,24,256]{3,0,2,1:T(4,128)S(1)} %get-tuple-element.19, f32[3,1,24,256]{3,0,2,1:T(4,128)S(1)} %get-tuple-element.20, f32[8]{0:T(128)S(1)} %pad.27.clone), kind=kLoop, calls=%fused_computation.29 | loop fusion | flops 147456 | bytes 368672 | tf_op jit(solution)/shard_map/squeeze | solution.py:256
  8.3 25.8 %shard_map.100 = (f32[3,26,8,256]{3,2,1,0:T(8,128)}, f32[10,24,256]{2,1,0:T(8,128)}, f32[10,2,8,128]{3,2,1,0:T(8,128)}, f32[16,2,8,128]{3,2,1,0:T(8,128)}) custom-call(f32[24,8,256]{2,1,0:T(8,128)} %maximum_bitcast_fusion.cells_ref, f32[24,256]{1,0:T(8,128)} %pad.12.coefs_ref, f32[2,8,128]{2,1,0:T(8,128)} %select_maximum_fusion.ends_ref, f32[8,128]{1,0:T(8,128)} %pad.14.share_ref), custom_call_target="tpu_custom_call" | custom-call | tf_op jit(solution)/shard_map/pallas_call | solution.py:198
  34.1 1.1 %copy-done.1 = f32[3,26,8,256]{3,2,1,0:T(8,128)S(1)} copy-done((f32[3,26,8,256]{3,2,1,0:T(8,128)S(1)}, f32[3,26,8,256]{3,2,1,0:T(8,128)}, u32[]{:S(2)}) %copy-start.1) | copy-done | bytes 639000
  35.2 29.9 %shard_map.101 = f32[24,8,256]{2,1,0:T(8,128)S(1)} custom-call(f32[3,26,8,256]{3,2,1,0:T(8,128)S(1)} %copy-done.1), custom_call_target="tpu_custom_call" | custom-call | flops 1415577600 | bytes 2555904 | tf_op jit(solution)/shard_map/pallas_call | solution.py:84
  65.1 0.0 copy-start.4
  65.2 0.1 select_reduce_fusion
  65.3 0.6 convolution_bitcast_fusion.1
  65.9 0.2 convolution_bitcast_fusion.2
  66.0 1.9 %fusion.17 = f32[3,24,64]{2,0,1:T(4,128)S(1)} fusion(f32[3,64,1]{1,0,2:T(4,128)S(1)} %convolution_bitcast_fusion.2, f32[1,24,64,64]{3,2,1,0:T(8,128)S(1)} %copy-done.2), kind=kOutput, calls=%fused_computation.18 | convolution fusion | flops 3538944 | bytes 412416 | tf_op jit(solution)/shard_map/slqk,rsk->rslq/dot_general | solution.py:290
  68.0 0.2 stack_reshape.3
  68.2 0.2 reshape.113
  68.4 0.0 copy-start.3
  68.4 0.1 fusion.24
  68.6 1.1 %copy-done.3 = f32[1,30,64,64]{3,2,1,0:T(8,128)S(1)} copy-done((f32[1,30,64,64]{3,2,1,0:T(8,128)S(1)}, f32[1,30,64,64]{3,2,1,0:T(8,128)}, u32[]{:S(2)}) %copy-start.3) | copy-done | bytes 491544
  69.6 1.2 %fusion.10 = f32[3,24,64]{2,1,0:T(8,128)S(1)} fusion(f32[10,1,24,3,64]{4,2,0,1,3:T(8,128)S(1)} %get-tuple-element.14, f32[10,1,24,3,64]{4,2,0,1,3:T(8,128)S(1)} %copy.27, f32[10,1,24,3,64]{4,2,0,1,3:T(8,128)S(1)} %get-tuple-element.13, f32[10,3,64,64]{3,2,1,0:T(8,128)S(1)} %bitcast.85, f32[10,3]{0,1:T(4,128)S(1)} %copy.28, f32[3,24,64]{2,0,1:T(4,128)S(1)} %fusion.17), kind=kOutput, calls=%fused_computation.7 | convolution fusion | flops 106572288 | bytes 1081464 | tf_op jit(solution)/shard_map/qbkz,qblrz->rlk/dot_general | solution.py:270
  70.8 0.9 %fusion.7 = f32[3,1,24,256]{3,0,2,1:T(4,128)S(1)} fusion(f32[1,24,64,256]{3,2,1,0:T(8,128)S(1)} %copy-done, f32[24,8,256]{2,1,0:T(8,128)S(1)} %shard_map.101, f32[3,24,64]{2,1,0:T(8,128)S(1)} %fusion.10), kind=kOutput, calls=%fused_computation.5 | convolution fusion | flops 14174208 | bytes 1738752 | tf_op jit(solution)/shard_map/slki,rslk->rsli/dot_general | solution.py:292
  71.7 0.6 copy.32
  (26 shorter events, 0.1 us)
Async XLA Ops:
  0.0 2.6 %copy-start = (f32[1,24,64,256]{3,2,1,0:T(8,128)S(1)}, f32[1,24,64,256]{3,2,1,0:T(8,128)}, u32[]{:S(2)}) copy-start(f32[1,24,64,256]{3,2,1,0:T(8,128)} %param.13) | copy-start | bytes 4718596
  0.0 5.4 %copy-start.8 = (f32[1,1,64,64]{3,2,1,0:T(8,128)S(1)}, f32[1,1,64,64]{3,2,1,0:T(8,128)}, u32[]{:S(2)}) copy-start(f32[1,1,64,64]{3,2,1,0:T(8,128)} %param.15) | copy-start | bytes 49156
  0.0 4.8 %copy-start.2 = (f32[1,24,64,64]{3,2,1,0:T(8,128)S(1)}, f32[1,24,64,64]{3,2,1,0:T(8,128)}, u32[]{:S(2)}) copy-start(f32[1,24,64,64]{3,2,1,0:T(8,128)} %param.14) | copy-start | bytes 1179652
  0.0 7.4 %copy-start.9 = (f32[1,24,256]{2,1,0:T(8,128)S(1)}, f32[1,24,256]{2,1,0:T(8,128)}, u32[]{:S(2)}) copy-start(f32[1,24,256]{2,1,0:T(8,128)} %param.12) | copy-start | bytes 73732
  0.0 7.4 %copy-start.6 = (f32[3,1,24,256]{3,2,1,0:T(8,128)S(1)}, f32[3,1,24,256]{3,2,1,0:T(8,128)}, u32[]{:S(2)}) copy-start(f32[3,1,24,256]{3,2,1,0:T(8,128)} %param.10) | copy-start | bytes 221188
  0.0 7.4 %copy-start.10 = (f32[3,1,24,256]{3,2,1,0:T(8,128)S(1)}, f32[3,1,24,256]{3,2,1,0:T(8,128)}, u32[]{:S(2)}) copy-start(f32[3,1,24,256]{3,2,1,0:T(8,128)} %param.11) | copy-start | bytes 221188
  34.1 1.1 %copy-start.1 = (f32[3,26,8,256]{3,2,1,0:T(8,128)S(1)}, f32[3,26,8,256]{3,2,1,0:T(8,128)}, u32[]{:S(2)}) copy-start(f32[3,26,8,256]{3,2,1,0:T(8,128)} %get-tuple-element.9.cells_ref) | copy-start | bytes 1916932
  35.1 29.9 %copy-start.11 = (f32[10,2,8,128]{3,2,1,0:T(8,128)S(1)}, f32[10,2,8,128]{3,2,1,0:T(8,128)}, u32[]{:S(2)}) copy-start(f32[10,2,8,128]{3,2,1,0:T(8,128)} %get-tuple-element.10) | copy-start | bytes 245764
  35.1 30.0 %copy-start.7 = (f32[16,2,8,128]{3,2,1,0:T(8,128)S(1)}, f32[16,2,8,128]{3,2,1,0:T(8,128)}, u32[]{:S(2)}) copy-start(f32[16,2,8,128]{3,2,1,0:T(8,128)} %get-tuple-element.12) | copy-start | bytes 393220
  35.1 30.1 %copy-start.5 = (f32[1,16,64,64]{3,2,1,0:T(8,128)S(1)}, f32[1,16,64,64]{3,2,1,0:T(8,128)}, u32[]{:S(2)}) copy-start(f32[1,16,64,64]{3,2,1,0:T(8,128)} %param.18) | copy-start | bytes 786436
  65.1 2.9 %copy-start.4 = (f32[10,24,256]{2,1,0:T(8,128)S(1)}, f32[10,24,256]{2,1,0:T(8,128)}, u32[]{:S(2)}) copy-start(f32[10,24,256]{2,1,0:T(8,128)} %get-tuple-element.11) | copy-start | bytes 737284
  68.4 1.2 %copy-start.3 = (f32[1,30,64,64]{3,2,1,0:T(8,128)S(1)}, f32[1,30,64,64]{3,2,1,0:T(8,128)}, u32[]{:S(2)}) copy-start(f32[1,30,64,64]{3,2,1,0:T(8,128)} %param.16) | copy-start | bytes 1474564

commit v3 on v2

--- a/solution.py
+++ b/solution.py
@@ -1,3 +1,5 @@
+import functools
+
 import jax
 import jax.numpy as jnp
 from jax import lax
@@ -18,7 +20,7 @@
     return high, x - high
 
 
-def near_kernel(cells_ref, out_ref, feature_ref, weight_ref):
+def near_steps(cells_ref, out_ref, feature_ref, weight_ref):
     leaves, _, size = out_ref.shape
     row = lax.broadcasted_iota(jnp.int32, (8, size), 0)
     log2e = 1.4426950408889634
@@ -41,10 +43,7 @@
 
         lax.fori_loop(0, leaves + 2, step, 0)
 
-    for a in range(3):
-        prepare(a)
-
-    def leaf(m, carry):
+    def leaf(sources, first, m, carry):
         cell = cells_ref[1, m + 1]
         high, low = split_in_two(jnp.where(row < 3, cell * (2 * SHARPNESS * log2e), 0.0))
         target = jnp.concatenate([high, high, low, low], 0).astype(jnp.bfloat16)
@@ -54,8 +53,8 @@
             * cell[6:7]
             * jnp.exp2((-SHARPNESS * log2e) * (x0 * x0 + x1 * x1 + x2 * x2))
         )
-        total = jnp.zeros((8, size), jnp.float32)
-        for a in range(3):
+        total = jnp.zeros((8, size), jnp.float32) if first else out_ref[m]
+        for a in sources:
             for b in range(3):
                 power = jnp.dot(
                     feature_ref[a, m + b], target, preferred_element_type=jnp.float32
@@ -74,27 +73,12 @@
         out_ref[m] = total
         return carry
 
-    lax.fori_loop(0, leaves, leaf, 0)
-
-
-def near_field(padded):
-    leaves = padded.shape[1] - 2
-    size = padded.shape[3]
-    tiles = 9 * leaves * size * size
-    return pl.pallas_call(
-        near_kernel,
-        out_shape=jax.ShapeDtypeStruct((leaves, 8, size), jnp.float32),
-        in_specs=[pl.BlockSpec(memory_space=pltpu.VMEM)],
-        out_specs=pl.BlockSpec(memory_space=pltpu.VMEM),
-        scratch_shapes=[
-            pltpu.VMEM((3, leaves + 2, size, 32), jnp.bfloat16),
-            pltpu.VMEM((3, leaves + 2, 3, 16, size), jnp.bfloat16),
-        ],
-        compiler_params=pltpu.CompilerParams(vmem_limit_bytes=40 * 1024 * 1024),
-        cost_estimate=pl.CostEstimate(
-            flops=100 * tiles, bytes_accessed=16 * padded.size, transcendentals=tiles
-        ),
-    )(padded)
+    def run(sources, first):
+        for a in sources:
+            prepare(a)
+        lax.fori_loop(0, leaves, functools.partial(leaf, sources, first), 0)
+
+    return run
 
 
 def far_offsets():
@@ -107,10 +91,13 @@
     coefs_ref,
     ends_ref,
     share_ref,
-    padded_ref,
+    near_ref,
     windows_ref,
     rims_ref,
     shares_ref,
+    padded_ref,
+    feature_ref,
+    weight_ref,
     send_sem,
     recv_sem,
     share_send_sem,
@@ -162,30 +149,48 @@
         share_copy(k, came, lax.rem(k, slabs)).wait_recv()
         return carry
 
-    lax.fori_loop(0, distant * slabs, share_start, 0)
+    for around in (0, -1, 1):
+        send(cells_ref.at[leaves - 1], padded_ref.at[1 - around, 0], around, 1)
+        send(cells_ref.at[0], padded_ref.at[1 - around, leaves + 1], around, -1)
     for around in (-1, 1):
         send(cells_ref, padded_ref.at[1 - around, pl.ds(1, leaves)], around, 0)
-    for around in (-1, 0, 1):
-        send(cells_ref.at[leaves - 1], padded_ref.at[1 - around, 0], around, 1)
-        send(cells_ref.at[0], padded_ref.at[1 - around, leaves + 1], around, -1)
+    lax.fori_loop(0, distant * slabs, share_start, 0)
     for q, around in enumerate(far_offsets()):
         send(coefs_ref, windows_ref.at[q], -around, 0)
         send(ends_ref.at[1], rims_ref.at[q, 0], -around, 1)
         send(ends_ref.at[0], rims_ref.at[q, 1], -around, -1)
     padded_ref[1, pl.ds(1, leaves)] = cells_ref[...]
-    for copy in copies:
+    run = near_steps(padded_ref, near_ref, feature_ref, weight_ref)
+
+    def close(a):
+        @pl.when(slab == 0)
+        def _():
+            padded_ref[a, 0] = jnp.zeros_like(padded_ref[a, 0])
+
+        @pl.when(slab == slabs - 1)
+        def _():
+            padded_ref[a, leaves + 1] = jnp.zeros_like(padded_ref[a, 0])
+
+    for copy in copies[:2]:
+        copy.wait()
+    close(1)
+    run((1,), True)
+    for copy in copies[2:8]:
+        copy.wait()
+    close(0)
+    close(2)
+    run((0, 2), False)
+    for copy in copies[8:]:
         copy.wait()
     lax.fori_loop(0, distant * slabs, share_wait, 0)
 
     @pl.when(slab == 0)
     def _():
-        padded_ref[:, 0] = jnp.zeros_like(padded_ref[:, 0])
         rims_ref[:, 0] = jnp.zeros_like(rims_ref[:, 0])
 
     @pl.when(slab == slabs - 1)
     def _():
-        padded_ref[:, leaves + 1] = jnp.zeros_like(padded_ref[:, 0])
-        rims_ref[:, 1] = jnp.zeros_like(rims_ref[:, 0])
+        rims_ref[:, 1] = jnp.zeros_like(rims_ref[:, 1])
 
 
 def exchange(cells, coefs, ends, share):
@@ -198,7 +203,7 @@
     return pl.pallas_call(
         exchange_kernel,
         out_shape=(
-            jax.ShapeDtypeStruct((3, leaves + 2, 8, size), jnp.float32),
+            jax.ShapeDtypeStruct((leaves, 8, size), jnp.float32),
             jax.ShapeDtypeStruct((far, *coefs.shape), jnp.float32),
             jax.ShapeDtypeStruct((far, *ends.shape), jnp.float32),
             jax.ShapeDtypeStruct((sectors, slabs, *share.shape), jnp.float32),
@@ -206,12 +211,17 @@
         in_specs=[vmem] * 4,
         out_specs=(vmem,) * 4,
         scratch_shapes=[
+            pltpu.VMEM((3, leaves + 2, 8, size), jnp.float32),
+            pltpu.VMEM((3, leaves + 2, size, 32), jnp.bfloat16),
+            pltpu.VMEM((3, leaves + 2, 3, 16, size), jnp.bfloat16),
             pltpu.SemaphoreType.DMA((links,)),
             pltpu.SemaphoreType.DMA((links,)),
             pltpu.SemaphoreType.DMA((pairs,)),
             pltpu.SemaphoreType.DMA((pairs,)),
         ],
-        compiler_params=pltpu.CompilerParams(has_side_effects=True),
+        compiler_params=pltpu.CompilerParams(
+            has_side_effects=True, vmem_limit_bytes=40 * 1024 * 1024
+        ),
     )(cells, coefs, ends, share)
 
 
@@ -252,13 +262,13 @@
     lanes = -(-rank // 128) * 128
     flat = by_leaf.reshape(leaves, count * rank)
     ends = jnp.stack([by_leaf[0], by_leaf[-1]])
-    padded, windows, rims, shares = exchange(
+    near, windows, rims, shares = exchange(
         cells[0],
         jnp.pad(flat, ((0, 0), (0, width - count * rank))),
         jnp.pad(ends, ((0, 0), (0, 8 - count), (0, lanes - rank))),
         jnp.pad(shared_portion[:, 0], ((0, 8 - count), (0, lanes - rank))),
     )
-    near = near_field(padded)[:, 3:6].transpose(1, 0, 2)[:, None]
+    near = near[:, 3:6].transpose(1, 0, 2)[:, None]
     far = windows.shape[0]
     windows = windows[:, :, : count * rank].reshape(far, leaves, count, rank)
     rims = rims[:, :, :count, :rank]

time: 72.7 us -> 61.8 us (0.85)
  Pallas kernels: 55.7 us -> 48.5 us
  local copies, waits for them, and re-layouts: 5.65 us -> 3.35 us
  other arithmetic: 3.14 us -> 1.88 us
    pallas_call x2 -> x1, Pallas kernels: 55.7 us -> 48.5 us  [exchange(): pl.pallas_call(exchange_kernel, out_shape=(jax.ShapeDtypeStruct((leaves,...]
    unnamed x24 -> x16, local copies, waits for them, and re-layouts: 2.18 us -> 1.09 us
where the time goes in v3:
time: 61.8 us; the launch traced here: 61.6 us
  Pallas kernels  48.5 us (78%)
  matrix products  7.66 us (12%)
  local copies, waits for them, and re-layouts  3.35 us (5%)
  other arithmetic  1.88 us (3%)
    pallas_call x1, Pallas kernels, exchange(): pl.pallas_call(exchange_kernel, out_shape=(jax.ShapeDtypeStruct((leaves,...  48.5 us
    dot_general x1, matrix products, body(): jnp.einsum('slki,rsli->rslk', leaf_basis, values, precision=HIGHEST_ACCUR...  2.26 us
    dot_general x1, matrix products, body(): jnp.einsum('slqk,rsk->rslq', transfer, slab_local_coefs, precision=HIGHES...  1.94 us

profile of v3, /device:TPU:0, one launch (start us, length us, event | category | flops | bytes accessed | tf_op | source)
XLA Modules:
  0.0 61.6 jit_solution(10763149204247725594)
XLA Ops:
  0.0 0.0 copy-start
  0.0 0.0 copy-start.4
  0.0 0.0 copy-start.7
  0.0 0.8 %convert_reduce_fusion = f32[30]{0:T(128)S(1)} fusion(s32[1,30]{1,0:T(1,128)} %param.17), kind=kLoop, calls=%fused_computation.49 | loop fusion | flops 30 | bytes 240 | tf_op jit(solution)/shard_map/convert_element_type | solution.py:278
  0.9 0.7 %bitcast_select_fusion = f32[16]{0:T(128)S(1)} fusion(s32[1,16]{1,0:T(1,128)} %param.19, s32[]{:T(128)S(6)} %axis_index.15), kind=kLoop, calls=%fused_computation.48 | loop fusion | flops 272 | bytes 132 | tf_op jit(solution)/shard_map/jit(_where)/select_n | solution.py:288
  1.5 0.1 pad.27.clone
  1.6 0.1 convert_element_type.27
  1.7 0.1 copy.28
  1.8 0.8 %broadcast_in_dim.27 = f32[1,1,24,256]{3,0,2,1:T(1,128)S(1)} reshape(f32[1,24,256]{2,1,0:T(8,128)} %param.12) | data formatting | bytes 49152 | tf_op jit(solution)/shard_map/broadcast_in_dim | solution.py:243
  2.6 2.3 %fusion.2 = f32[24,3,64]{2,1,0:T(4,128)S(1)} fusion(f32[1,24,64,256]{3,2,1,0:T(8,128)S(1)} %copy-done, f32[3,24,256]{2,1,0:T(8,128)} %bitcast.86), kind=kOutput, calls=%fused_computation.2 | convolution fusion | flops 14155776 | bytes 1665024 | tf_op jit(solution)/shard_map/slki,rsli->rslk/dot_general | solution.py:249
  4.8 0.0 copy-done.1
  4.8 0.5 convolution_bitcast_fusion.3
  5.4 0.1 fusion.30
  5.5 0.1 reshape.109
  5.6 0.0 copy-done.6
  5.7 0.0 copy-done.4
  5.7 0.0 copy-done.7
  5.7 0.1 copy_multiply_fusion.2
  5.8 0.1 maximum_bitcast_fusion.cells_ref
  5.9 48.5 %shard_map.100 = (f32[24,8,256]{2,1,0:T(8,128)S(1)}, f32[10,24,256]{2,1,0:T(8,128)S(1)}, f32[10,2,8,128]{3,2,1,0:T(8,128)S(1)}, f32[16,2,8,128]{3,2,1,0:T(8,128)S(1)}) custom-call(f32[24,8,256]{2,1,0:T(8,128)S(1)} %maximum_bitcast_fusion.cells_ref, f32[24,256]{1,0:T(8,128)S(1)} %pad.12.coefs_ref, f32[2,8,128]{2,1,0:T(8,128)S(1)} %select_maximum_fusion.ends_ref, ...), custom_call_target="tpu_custom_call" | custom-call | tf_op jit(solution)/shard_map/pallas_call | solution.py:203
  54.4 0.1 select_reduce_fusion
  54.5 0.6 convolution_bitcast_fusion.1
  55.1 0.2 convolution_bitcast_fusion.2
  55.3 1.9 %fusion.17 = f32[3,24,64]{2,0,1:T(4,128)S(1)} fusion(f32[3,64,1]{1,0,2:T(4,128)S(1)} %convolution_bitcast_fusion.2, f32[1,24,64,64]{3,2,1,0:T(8,128)S(1)} %copy-done.1), kind=kOutput, calls=%fused_computation.18 | convolution fusion | flops 3538944 | bytes 412416 | tf_op jit(solution)/shard_map/slqk,rsk->rslq/dot_general | solution.py:300
  57.2 0.2 stack_reshape.3
  57.5 0.2 reshape.113
  57.7 0.0 copy-start.2
  57.7 0.1 fusion.24
  57.8 1.1 %copy-done.2 = f32[1,30,64,64]{3,2,1,0:T(8,128)S(1)} copy-done((f32[1,30,64,64]{3,2,1,0:T(8,128)S(1)}, f32[1,30,64,64]{3,2,1,0:T(8,128)}, u32[]{:S(2)}) %copy-start.2) | copy-done | bytes 491544
  58.9 1.2 %fusion.10 = f32[3,24,64]{2,1,0:T(8,128)S(1)} fusion(f32[10,1,24,3,64]{4,2,0,1,3:T(8,128)S(1)} %get-tuple-element.14, f32[10,1,24,3,64]{4,2,0,1,3:T(8,128)S(1)} %copy.27, f32[10,1,24,3,64]{4,2,0,1,3:T(8,128)S(1)} %get-tuple-element.13, f32[10,3,64,64]{3,2,1,0:T(8,128)S(1)} %bitcast.85, f32[10,3]{0,1:T(4,128)S(1)} %copy.28, f32[3,24,64]{2,0,1:T(4,128)S(1)} %fusion.17), kind=kOutput, calls=%fused_computation.7 | convolution fusion | flops 106572288 | bytes 1081464 | tf_op jit(solution)/shard_map/qbkz,qblrz->rlk/dot_general | solution.py:280
  60.0 0.9 %fusion.7 = f32[3,1,24,256]{3,0,2,1:T(4,128)S(1)} fusion(f32[1,24,64,256]{3,2,1,0:T(8,128)S(1)} %copy-done, f32[24,8,256]{2,1,0:T(8,128)S(1)} %get-tuple-element.9, f32[3,24,64]{2,1,0:T(8,128)S(1)} %fusion.10), kind=kOutput, calls=%fused_computation.5 | convolution fusion | flops 14174208 | bytes 1738752 | tf_op jit(solution)/shard_map/slki,rslk->rsli/dot_general | solution.py:302
  60.9 0.6 %copy.32 = f32[3,1,24,256]{3,2,1,0:T(8,128)} copy(f32[3,1,24,256]{3,0,2,1:T(4,128)S(1)} %fusion.7) | data formatting | bytes 147456 | tf_op jit(solution)/shard_map/add | solution.py:302
  (17 shorter events, 0.1 us)
Async XLA Ops:
  0.0 2.6 %copy-start = (f32[1,24,64,256]{3,2,1,0:T(8,128)S(1)}, f32[1,24,64,256]{3,2,1,0:T(8,128)}, u32[]{:S(2)}) copy-start(f32[1,24,64,256]{3,2,1,0:T(8,128)} %param.13) | copy-start | bytes 4718596
  0.0 5.4 %copy-start.5 = (f32[1,1,64,64]{3,2,1,0:T(8,128)S(1)}, f32[1,1,64,64]{3,2,1,0:T(8,128)}, u32[]{:S(2)}) copy-start(f32[1,1,64,64]{3,2,1,0:T(8,128)} %param.15) | copy-start | bytes 49156
  0.0 4.8 %copy-start.1 = (f32[1,24,64,64]{3,2,1,0:T(8,128)S(1)}, f32[1,24,64,64]{3,2,1,0:T(8,128)}, u32[]{:S(2)}) copy-start(f32[1,24,64,64]{3,2,1,0:T(8,128)} %param.14) | copy-start | bytes 1179652
  0.0 5.6 %copy-start.6 = (f32[1,24,256]{2,1,0:T(8,128)S(1)}, f32[1,24,256]{2,1,0:T(8,128)}, u32[]{:S(2)}) copy-start(f32[1,24,256]{2,1,0:T(8,128)} %param.12) | copy-start | bytes 73732
  0.0 5.6 %copy-start.4 = (f32[3,1,24,256]{3,2,1,0:T(8,128)S(1)}, f32[3,1,24,256]{3,2,1,0:T(8,128)}, u32[]{:S(2)}) copy-start(f32[3,1,24,256]{3,2,1,0:T(8,128)} %param.10) | copy-start | bytes 221188
  0.0 5.6 %copy-start.7 = (f32[3,1,24,256]{3,2,1,0:T(8,128)S(1)}, f32[3,1,24,256]{3,2,1,0:T(8,128)}, u32[]{:S(2)}) copy-start(f32[3,1,24,256]{3,2,1,0:T(8,128)} %param.11) | copy-start | bytes 221188
  4.8 49.7 %copy-start.3 = (f32[1,16,64,64]{3,2,1,0:T(8,128)S(1)}, f32[1,16,64,64]{3,2,1,0:T(8,128)}, u32[]{:S(2)}) copy-start(f32[1,16,64,64]{3,2,1,0:T(8,128)} %param.18) | copy-start | bytes 786436
  57.7 1.2 %copy-start.2 = (f32[1,30,64,64]{3,2,1,0:T(8,128)S(1)}, f32[1,30,64,64]{3,2,1,0:T(8,128)}, u32[]{:S(2)}) copy-start(f32[1,30,64,64]{3,2,1,0:T(8,128)} %param.16) | copy-start | bytes 1474564
